TPU v7x, 512 devices: a whole 4x8x8 slice. The times are simulated.
512 devices in a mesh: dp: 64 (over z, y), tensor: 8 (over x, core).
Axes of the slice: x: 4, y: 8, z: 8, core: 2. Of those that a mesh axis runs over, the one named last changes fastest.
Arguments:
- tokens: bfloat16 [8192, 2048], P('dp'), may hold values from -8 to 8
- grad_out: bfloat16 [8192, 2048], P('dp'), may hold values from -6 to 6
- route_ids: int32 [8192, 4], P('dp'), may hold values from 0 to 59, as said below
- expert_map: int32 [60], replicated, may hold values from 0 to 63, as said below
- router: bfloat16 [2048, 60], replicated, may hold values from -1 to 1
- shared_gate: bfloat16 [2048], replicated, may hold values from -0.125 to 0.125
- sh_gate: bfloat16 [2048, 2816], P('dp', 'tensor'), may hold values from -0.125 to 0.125
- sh_up: bfloat16 [2048, 2816], P('dp', 'tensor'), may hold values from -0.125 to 0.125
- sh_down: bfloat16 [2816, 2048], P('tensor', 'dp'), may hold values from -0.109375 to 0.109375
- ex_gate: bfloat16 [64, 2048, 1408], P('dp', None, 'tensor'), may hold values from -0.125 to 0.125
- ex_up: bfloat16 [64, 2048, 1408], P('dp', None, 'tensor'), may hold values from -0.125 to 0.125
- ex_down: bfloat16 [64, 1408, 2048], P('dp', 'tensor'), may hold values from -0.15625 to 0.15625
Outputs:
- mixed: bfloat16 [8192, 2048], P('dp', 'tensor')
- grad_tokens: bfloat16 [8192, 2048], P('dp', 'tensor')
Inputs may be any that keep to these rules, and one draw needn't show every extreme that they name: `route_ids`: each row names 4 different experts. Within the rows of one device (aligned blocks of 128 rows), no expert is named more than 9 times over all 4 columns, and some expert is named exactly 9 times. Entries are distinct. Expert e uses the weights of slot expert_map[e]; slot s is held by index s // 1 of dp. Slots that no expert names are not used.
All inputs are finite; a program needn't handle non-finite values.
Results may differ from a plain program's by a relative error of at most 0.011.
Values may be sent and summed in bfloat16 or wider, within the bound.
A program may use at most 64 MiB of HBM per device.

v0:
```python
import jax
import jax.numpy as jnp
from jax import lax
from jax.sharding import PartitionSpec as P

CAP = 9


def turned_gather(arrays, axis, dims):
    turned = [jnp.moveaxis(a, dim, 0) for a, dim in zip(arrays, dims)]
    both = jnp.concatenate([t.reshape(len(t), -1) for t in turned], axis=1)
    result, at, outs = (lax.all_gather(both, axis, axis=0, tiled=True), 0, [])
    for t, dim in zip(turned, dims):
        share = result[:, at : at + t[0].size].reshape(-1, *t.shape[1:])
        outs.append(jnp.moveaxis(share, 0, dim))
        at += t[0].size
    return tuple(outs)


def in_one_piece(arrays, axis, split_dim, concat_dim, along):
    ends, at = ([], 0)
    for a in arrays[:-1]:
        at += a.shape[along]
        ends.append(at)
    both = jnp.concatenate(arrays, axis=along)
    return tuple(
        jnp.split(
            lax.all_to_all(both, axis, split_axis=split_dim, concat_axis=concat_dim, tiled=True),
            ends,
            axis=along,
        )
    )


def in_one_piece_2(arrays, axis, dim, along):
    ends, at = ([], 0)
    for a in arrays[:-1]:
        at += a.shape[along]
        ends.append(at)
    both = jnp.concatenate(arrays, axis=along)
    return tuple(jnp.split(lax.all_gather(both, axis, axis=dim, tiled=True), ends, axis=along))


def copy_for_each(x, axis):
    peers = lax.axis_size(axis)
    return lax.all_to_all(jnp.broadcast_to(x[None], (peers, *x.shape)), axis, 0, 0, tiled=True)


def of_everyone(x, axis):
    return copy_for_each(x, axis).sum(axis=0)


def together(arrays, axis):
    line, at, outs = (jnp.concatenate([a.reshape(-1) for a in arrays]), 0, [])
    subtotal = of_everyone(line, axis)
    for a in arrays:
        outs.append(subtotal[at : at + a.size].reshape(a.shape))
        at += a.size
    return tuple(outs)


def side_by_side(arrays, axis, dim, along):
    ends, at = ([], 0)
    for a in arrays[:-1]:
        at += a.shape[along]
        ends.append(at)
    both = jnp.concatenate(arrays, axis=along)
    return tuple(
        jnp.split(lax.psum_scatter(both, axis, scatter_dimension=dim, tiled=True), ends, axis=along)
    )


def silu_pair(pre_gate):
    sigmoid_val = 1.0 / (1.0 + jnp.exp(-pre_gate))
    return (pre_gate * sigmoid_val, sigmoid_val * (1.0 + pre_gate * (1.0 - sigmoid_val)))


def contract_last(left, right):
    return lax.dot_general(
        left, right, (((1,), (1,)), ((), ())), preferred_element_type=jnp.float32
    )


def expert_block(rows_in, rows_cot, w_gate, w_up, w_down):
    pre_gate = jnp.dot(rows_in, w_gate, preferred_element_type=jnp.float32)
    pre_up = jnp.dot(rows_in, w_up, preferred_element_type=jnp.float32)
    active, derivative = silu_pair(pre_gate)
    hidden = (active * pre_up).astype(jnp.bfloat16)
    result = jnp.dot(hidden, w_down, preferred_element_type=jnp.float32)
    grad_hidden = contract_last(rows_cot, w_down)
    grad_gate = (grad_hidden * pre_up * derivative).astype(jnp.bfloat16)
    grad_up = (grad_hidden * active).astype(jnp.bfloat16)
    backward = contract_last(grad_gate, w_gate) + contract_last(grad_up, w_up)
    return (result, backward)


def expert_batch(rows_in, rows_cot, w_gate, w_up, w_down):
    pre_gate = jnp.einsum("slcd,ldf->slcf", rows_in, w_gate, preferred_element_type=jnp.float32)
    pre_up = jnp.einsum("slcd,ldf->slcf", rows_in, w_up, preferred_element_type=jnp.float32)
    active, derivative = silu_pair(pre_gate)
    hidden = (active * pre_up).astype(jnp.bfloat16)
    result = jnp.einsum(
        "slcf,lfd->slcd", hidden, w_down, preferred_element_type=jnp.float32
    ).astype(jnp.bfloat16)
    grad_hidden = jnp.einsum("slcd,lfd->slcf", rows_cot, w_down, preferred_element_type=jnp.float32)
    grad_gate = (grad_hidden * pre_up * derivative).astype(jnp.bfloat16)
    grad_up = (grad_hidden * active).astype(jnp.bfloat16)
    grad_both = jnp.concatenate([grad_gate, grad_up], axis=3)
    weight_both = jnp.concatenate([w_gate, w_up], axis=2)
    backward = jnp.einsum(
        "slcf,ldf->slcd", grad_both, weight_both, preferred_element_type=jnp.float32
    )
    return (result, backward.astype(jnp.bfloat16))


def shards(
    tokens,
    grad_out,
    route_ids,
    expert_map,
    router,
    shared_gate,
    sh_gate,
    sh_up,
    sh_down,
    ex_gate,
    ex_up,
    ex_down,
):
    tok_dev, width = tokens.shape
    top_count = route_ids.shape[1]
    expert_count = router.shape[1]
    dp_size = lax.axis_size("dp")
    tensor_size = lax.axis_size("tensor")
    tensor_rank = lax.axis_index("tensor")
    local_slots = ex_gate.shape[0]
    col_width = width // tensor_size
    col_start = tensor_rank * col_width
    buffer_rows = dp_size * local_slots * CAP
    slot_rows = local_slots * CAP
    flat_ids = route_ids.reshape(-1)
    chosen = (flat_ids[:, None] == jnp.arange(expert_count, dtype=jnp.int32)[None, :]).astype(
        jnp.int32
    )
    earlier = jnp.sum((jnp.cumsum(chosen, axis=0) - chosen) * chosen, axis=1)
    slot_of = jnp.sum(chosen * expert_map[None, :], axis=1)
    position = slot_of * CAP + earlier
    token_index = jnp.arange(tok_dev * top_count, dtype=jnp.int32) // top_count
    source_rows = jnp.full((buffer_rows,), tok_dev, jnp.int32).at[position].set(token_index)

    def fetch_rows(table):
        padded = jnp.concatenate([table, jnp.zeros((1, table.shape[1]), table.dtype)], axis=0)
        return jnp.take(padded, source_rows, axis=0)

    def run_routed():
        part_in = lax.dynamic_slice_in_dim(tokens, col_start, col_width, 1)
        part_cot = lax.dynamic_slice_in_dim(grad_out, col_start, col_width, 1)
        send_in = fetch_rows(part_in).reshape(dp_size, slot_rows, col_width)
        send_cot = fetch_rows(part_cot).reshape(dp_size, slot_rows, col_width)
        got_in, got_cot = in_one_piece((send_in, send_cot), "dp", 0, 0, 1)
        got_in, got_cot = in_one_piece_2((got_in, got_cot), "tensor", 2, 0)
        grid_shape = (dp_size, local_slots, CAP, width)
        result, backward = expert_batch(
            got_in.reshape(grid_shape), got_cot.reshape(grid_shape), ex_gate, ex_up, ex_down
        )
        split_out = result.reshape(buffer_rows, tensor_size, col_width)
        split_back = backward.reshape(buffer_rows, tensor_size, col_width)
        met_out, met_back = in_one_piece((split_out, split_back), "tensor", 1, 1, 0)
        summed_out = jnp.sum(met_out.astype(jnp.float32), axis=1).reshape(
            dp_size, slot_rows, col_width
        )
        summed_back = jnp.sum(met_back.astype(jnp.float32), axis=1).reshape(
            dp_size, slot_rows, col_width
        )
        came_out, came_back = tuple(
            (
                part.astype(jnp.float32)
                for part in in_one_piece(
                    (summed_out.astype(jnp.bfloat16), summed_back.astype(jnp.bfloat16)),
                    "dp",
                    0,
                    0,
                    1,
                )
            )
        )
        return (came_out.reshape(buffer_rows, col_width), came_back.reshape(buffer_rows, col_width))

    routed_out, routed_back = run_routed()
    weights = turned_gather((sh_gate, sh_up, sh_down), "dp", (0, 0, 1))
    full_gate, full_up, full_down = weights
    sh_out, sh_back = expert_block(tokens, grad_out, full_gate, full_up, full_down)
    routed_width = routed_out.shape[1]
    expert_out = jnp.take(routed_out, position, axis=0).reshape(tok_dev, top_count, routed_width)
    expert_back = jnp.take(routed_back, position, axis=0).reshape(tok_dev, top_count, routed_width)
    logits = jnp.dot(tokens, router, preferred_element_type=jnp.float32)
    exp_logit = jnp.exp(logits)
    prob_table = exp_logit / jnp.sum(exp_logit, axis=1, keepdims=True)
    picked = chosen.reshape(tok_dev, top_count, expert_count).astype(jnp.float32)
    gate_weights = jnp.sum(picked * prob_table[:, None, :], axis=2)
    shared_scale = 1.0 / (
        1.0 + jnp.exp(-jnp.dot(tokens, shared_gate, preferred_element_type=jnp.float32))
    )
    shared_part = jnp.sum(grad_out.astype(jnp.float32) * sh_out, axis=1)
    cot_cols = lax.dynamic_slice_in_dim(grad_out, col_start, col_width, 1).astype(jnp.float32)
    dots_part = jnp.sum(cot_cols[:, None, :] * expert_out, axis=2)
    routed_mixed = jnp.sum(gate_weights[:, :, None] * expert_out, axis=1)
    routed_grad = jnp.sum(gate_weights[:, :, None] * expert_back, axis=1)
    mixed_part = shared_scale[:, None] * sh_out
    grad_part = shared_scale[:, None] * sh_back
    out_dots, shared_dots = together((dots_part, shared_part), "tensor")
    mixed_cols, grad_cols = tuple(
        (
            part.astype(jnp.float32)
            for part in side_by_side(
                (mixed_part.astype(jnp.bfloat16), grad_part.astype(jnp.bfloat16)), "tensor", 1, 0
            )
        )
    )
    mixed_cols = mixed_cols + routed_mixed
    grad_cols = grad_cols + routed_grad
    grad_prob = jnp.sum(picked * out_dots[:, :, None], axis=1)
    dlogits = prob_table * (grad_prob - jnp.sum(gate_weights * out_dots, axis=1, keepdims=True))
    router_cols = lax.dynamic_slice_in_dim(router, col_start, col_width, 0).astype(jnp.float32)
    grad_router = lax.dot_general(
        dlogits,
        router_cols,
        (((1,), (1,)), ((), ())),
        precision=lax.Precision.HIGHEST,
        preferred_element_type=jnp.float32,
    )
    gate_cols = lax.dynamic_slice_in_dim(shared_gate, col_start, col_width, 0).astype(jnp.float32)
    slope_term = shared_dots * shared_scale * (1.0 - shared_scale)
    grad_total = grad_cols + grad_router + slope_term[:, None] * gate_cols[None, :]
    return (mixed_cols.astype(jnp.bfloat16), grad_total.astype(jnp.bfloat16))


def solution(mesh):
    placed = (
        P("dp", None),
        P("dp", None),
        P("dp", None),
        P(),
        P(),
        P(),
        P("dp", "tensor"),
        P("dp", "tensor"),
        P("tensor", "dp"),
        P("dp", None, "tensor"),
        P("dp", None, "tensor"),
        P("dp", "tensor", None),
    )
    return jax.shard_map(
        shards,
        mesh=mesh,
        in_specs=placed,
        out_specs=(P("dp", "tensor"), P("dp", "tensor")),
        check_vma=False,
    )
```

profile of v0, /device:TPU:1, one launch (start us, length us, event | category | flops | bytes accessed | tf_op | source)
XLA Modules:
  0.0 265.0 jit_solution(9257027790201195252)
XLA Ops:
  8.3 1.2 reduce-window.6
  10.8 2.4 scatter_custom_fusion
  14.3 2.7 %gather_fusion.1 = bf16[576,256]{1,0:T(8,128)(2,1)S(1)} fusion(bf16[129,256]{1,0:T(8,128)(2,1)S(1)} %concatenate.36, s32[1024]{0:T(1024)S(1)} %pad_clamp_fusion.1), kind=kCustom, calls=%fused_computation.2.clone | custom fusion | bytes 592128 | tf_op jit(solution)/shard_map/jit(_take)/gather | solution.py:153
  17.0 2.7 %gather_fusion = bf16[576,256]{1,0:T(8,128)(2,1)S(1)} fusion(bf16[129,256]{1,0:T(8,128)(2,1)S(1)} %concatenate.35, s32[1024]{0:T(1024)S(1)} %pad_clamp_fusion.1), kind=kCustom, calls=%fused_computation.clone | custom fusion | bytes 592128 | tf_op jit(solution)/shard_map/jit(_take)/gather | solution.py:153
  20.4 38.9 %all_to_all.21 = bf16[64,18,256]{2,1,0:T(8,128)(2,1)S(1)} all-to-all(bf16[64,18,256]{2,1,0:T(8,128)(2,1)S(1)} %pad_maximum_fusion.2), channel_id=1, replica_groups=mesh['dp'=64,'tensor'=8] {'dp'}, dimensions={0} | all-to-all | bytes 1179648 | tf_op jit(solution)/shard_map/all_to_all | solution.py:28
  61.6 39.5 %all-gather.5.cloned.1.call-done = bf16[128,9,2048]{2,0,1:T(8,128)(2,1)} async-done(((bf16[128,9,256]{2,0,1:T(8,128)(2,1)}), bf16[128,9,2048]{2,0,1:T(8,128)(2,1)}) %all-gather.5.cloned.1.call-update) | async-done | bytes 4718608 | tf_op jit(solution)/shard_map/all_gather | solution.py:41
  101.1 2.6 fusion.26
  105.3 1.8 multiply_convert_fusion.2
  107.9 3.5 %copy.52 = bf16[64,1,9,2048]{3,2,0,1:T(8,128)(2,1)} copy(bf16[64,1,9,2048]{3,0,2,1:T(8,128)(2,1)S(1)} %fusion) | data formatting | bytes 4718592 | tf_op jit(solution)/shard_map/convert_element_type | solution.py:104
  111.4 4.4 %reshape.172 = bf16[576,8,256]{2,1,0:T(8,128)(2,1)S(1)} reshape(bf16[64,1,9,2048]{3,2,0,1:T(8,128)(2,1)} %copy.52) | data formatting | bytes 4718592 | tf_op jit(solution)/shard_map/reshape | solution.py:166
  115.9 2.7 %fusion.1 = bf16[64,1,9,2048]{3,0,2,1:T(8,128)(2,1)S(1)} fusion(bf16[1,2048,176]{1,2,0:T(8,128)(2,1)S(1)} %copy-done.13, bf16[1,2048,176]{1,2,0:T(8,128)(2,1)} %param.25, bf16[64,1,9,176]{3,0,2,1:T(8,128)(2,1)} %get-tuple-element.17, bf16[64,1,9,176]{3,0,2,1:T(8,128)(2,1)} %get-tuple-element.16), kind=kOutput, calls=%fused_computation.9 | convolution fusion | flops 835346432 | bytes 4206592 | tf_op jit(solution)/shard_map/slcf,ldf->slcd/dot_general | solution.py:110
  118.6 3.5 %copy.53 = bf16[64,1,9,2048]{3,2,0,1:T(8,128)(2,1)} copy(bf16[64,1,9,2048]{3,0,2,1:T(8,128)(2,1)S(1)} %fusion.1) | data formatting | bytes 4718592 | tf_op jit(solution)/shard_map/convert_element_type | solution.py:113
  122.1 5.8 %reshape.175 = bf16[576,8,256]{2,1,0:T(8,128)(2,1)} reshape(bf16[64,1,9,2048]{3,2,0,1:T(8,128)(2,1)} %copy.53) | data formatting | bytes 4718592 | tf_op jit(solution)/shard_map/reshape | solution.py:167
  128.0 4.6 %pad_maximum_fusion = bf16[1152,8,256]{2,1,0:T(8,128)(2,1)S(1)} fusion(bf16[576,8,256]{2,1,0:T(8,128)(2,1)} %reshape.175, bf16[576,8,256]{2,1,0:T(8,128)(2,1)S(1)} %reshape.172), kind=kLoop, calls=%fused_computation.5 | loop fusion | flops 2359296 | bytes 9437184 | tf_op jit(solution)/shard_map/concatenate | solution.py:25
  132.6 3.2 %copy.54 = bf16[1152,8,256]{2,0,1:T(8,128)(2,1)} copy(bf16[1152,8,256]{2,1,0:T(8,128)(2,1)S(1)} %pad_maximum_fusion) | data formatting | bytes 9437184 | tf_op jit(solution)/shard_map/concatenate | solution.py:25
  135.7 5.1 %all-to-all-start.1 = ((bf16[1152,8,256]{2,0,1:T(8,128)(2,1)}), bf16[1152,8,256]{2,0,1:T(8,128)(2,1)}, u32[]{:S(2)}, u32[]{:S(2)}) async-start(bf16[1152,8,256]{2,0,1:T(8,128)(2,1)} %copy.54), calls=%async_computation.2 | async-start | bytes 9437184 | tf_op jit(solution)/shard_map/all_to_all | solution.py:28
  141.1 46.9 %all-gather.3.cloned.1.call-done = bf16[2048,1056]{1,0:T(8,128)(2,1)} async-done(((bf16[32,1056]{1,0:T(8,128)(2,1)}), bf16[2048,1056]{1,0:T(8,128)(2,1)}) %all-gather.3.cloned.1.call-update) | async-done | bytes 4325392 | tf_op jit(solution)/shard_map/all_gather | solution.py:12
  188.0 2.1 fusion.32
  190.2 2.7 %fusion.35 = f32[128,352]{0,1:T(8,128)S(1)} fusion(bf16[128,2048]{1,0:T(8,128)(2,1)S(1)} %copy-done.2, bf16[2048,1056]{1,0:T(8,128)(2,1)} %all-gather.3.cloned.1.call-done), kind=kOutput, calls=%fused_computation.39 | convolution fusion | flops 184549376 | bytes 2277376 | tf_op jit(solution)/shard_map/dot_general | solution.py:86
  195.7 3.7 %slice_reduce_fusion.1 = (bf16[576,256]{1,0:T(8,128)(2,1)S(1)}, bf16[576,256]{1,0:T(8,128)(2,1)S(1)}) fusion(bf16[1152,8,256]{2,0,1:T(8,128)(2,1)} %all-to-all-done.1), kind=kLoop, calls=%fused_computation.14 | loop fusion | flops 2064384 | bytes 5308416 | tf_op jit(solution)/shard_map/reduce_sum | solution.py:169
  200.8 12.6 %all-to-all-start.2 = ((bf16[64,18,256]{2,1,0:T(8,128)(2,1)}), bf16[64,18,256]{2,1,0:T(8,128)(2,1)S(1)}, u32[]{:S(2)}, u32[]{:S(2)}) async-start(bf16[64,18,256]{2,1,0:T(8,128)(2,1)} %pad_maximum_fusion.3), calls=%async_computation.3 | async-start | bytes 1572864 | tf_op jit(solution)/shard_map/all_to_all | solution.py:28
  213.4 2.8 %multiply_convert_fusion = (bf16[128,2048]{1,0:T(8,128)(2,1)S(1)}, f32[128]{0:T(128)S(1)}) fusion(f32[128]{0:T(128)S(1)} %fusion.46, bf16[128,2048]{1,0:T(8,128)(2,1)} %param.17, bf16[2048,1056]{1,0:T(8,128)(2,1)} %all-gather.3.cloned.1.call-done, f32[128,352]{0,1:T(8,128)S(1)} %fusion.35, f32[128,352]{0,1:T(8,128)S(1)} %fusion.32), kind=kOutput, calls=%fused_computation.52 | convolution fusion | flops 186130304 | bytes 2982912 | tf_op jit(solution)/shard_map/dot_general | solution.py:89
  217.9 16.9 %all-to-all-done.2 = bf16[64,18,256]{2,1,0:T(8,128)(2,1)S(1)} async-done(((bf16[64,18,256]{2,1,0:T(8,128)(2,1)}), bf16[64,18,256]{2,1,0:T(8,128)(2,1)S(1)}, u32[]{:S(2)}, u32[]{:S(2)}) %all-to-all-start.2) | async-done | bytes 589856 | tf_op jit(solution)/shard_map/all_to_all | solution.py:28
  234.8 1.3 slice_convert_fusion.1
  236.1 1.3 reshape.185
  237.6 1.6 gather_fusion.3
  239.2 1.6 gather_fusion.2
  242.4 6.9 %all-to-all-start.3 = ((f32[8,1,640]{2,1,0:T(1,128)}), f32[8,1,640]{2,1,0:T(1,128)S(1)}, u32[]{:S(2)}, u32[]{:S(2)}) async-start(f32[8,1,640]{2,1,0:T(1,128)} %broadcast_in_dim.23), calls=%async_computation.4 | async-start | bytes 40960 | tf_op jit(solution)/shard_map/all_to_all | solution.py:46
  249.4 1.2 reshape.178
  250.7 3.3 %all-to-all-done.3 = f32[8,1,640]{2,1,0:T(1,128)S(1)} async-done(((f32[8,1,640]{2,1,0:T(1,128)}), f32[8,1,640]{2,1,0:T(1,128)S(1)}, u32[]{:S(2)}, u32[]{:S(2)}) %all-to-all-start.3) | async-done | bytes 20512 | tf_op jit(solution)/shard_map/all_to_all | solution.py:46
  255.2 1.5 add_convert_fusion
  256.7 1.7 fusion.42
  (100 shorter events, 17.8 us)
Async XLA Ops:
  7.2 96.6 %copy-start = (bf16[1,176,2048]{2,1,0:T(8,128)(2,1)S(1)}, bf16[1,176,2048]{2,1,0:T(8,128)(2,1)}, u32[]{:S(2)}) copy-start(bf16[1,176,2048]{2,1,0:T(8,128)(2,1)} %param.27) | copy-start | bytes 2162692
  7.2 93.9 %all-gather.5.cloned.1.call-start = ((), (), s32[]{:S(2)}) async-start(), calls=%async_computation.7 | async-start | bytes 5308416 | tf_op jit(solution)/shard_map/all_gather | solution.py:41
  59.3 1.5 copy-start.5
  59.3 1.5 copy-start.6
  59.3 1.6 copy-start.7
  59.3 41.8 %copy-start.12 = (bf16[1,2048,176]{1,2,0:T(8,128)(2,1)S(1)}, bf16[1,2048,176]{1,2,0:T(8,128)(2,1)}, u32[]{:S(2)}) copy-start(bf16[1,2048,176]{1,2,0:T(8,128)(2,1)} %param.26) | copy-start | bytes 2162692
  60.6 127.4 %all-gather.3.cloned.1.call-start = ((), (), s32[]{:S(2)}) async-start(), calls=%async_computation.5 | async-start | bytes 4792320 | tf_op jit(solution)/shard_map/all_gather | solution.py:12
  101.1 3.0 %copy-start.11 = (bf16[128,9,2048]{2,0,1:T(8,128)(2,1)S(1)}, bf16[128,9,2048]{2,0,1:T(8,128)(2,1)}, u32[]{:S(2)}) copy-start(bf16[128,9,2048]{2,0,1:T(8,128)(2,1)} %all-gather.5.cloned.1.call-done) | copy-start | bytes 14155780
  104.2 1.1 copy-start.14
  111.4 4.4 %copy-start.13 = (bf16[1,2048,176]{1,2,0:T(8,128)(2,1)S(1)}, bf16[1,2048,176]{1,2,0:T(8,128)(2,1)}, u32[]{:S(2)}) copy-start(bf16[1,2048,176]{1,2,0:T(8,128)(2,1)} %param.26) | copy-start | bytes 2162692
  135.7 5.1 %copy-start.10 = (bf16[2048]{0:T(1024)(128)(2,1)S(1)}, bf16[2048]{0:T(1024)(128)(2,1)}, u32[]{:S(2)}) copy-start(bf16[2048]{0:T(1024)(128)(2,1)} %param.21) | copy-start | bytes 12292
  135.7 5.1 %copy-start.2 = (bf16[128,2048]{1,0:T(8,128)(2,1)S(1)}, bf16[128,2048]{1,0:T(8,128)(2,1)}, u32[]{:S(2)}) copy-start(bf16[128,2048]{1,0:T(8,128)(2,1)} %param.16) | copy-start | bytes 1572868
  135.7 59.9 %all-to-all-start.1 = ((bf16[1152,8,256]{2,0,1:T(8,128)(2,1)}), bf16[1152,8,256]{2,0,1:T(8,128)(2,1)}, u32[]{:S(2)}, u32[]{:S(2)}) async-start(bf16[1152,8,256]{2,0,1:T(8,128)(2,1)} %copy.54), calls=%async_computation.2 | async-start | bytes 9437184 | tf_op jit(solution)/shard_map/all_to_all | solution.py:28
  141.1 51.7 %copy-start.9 = (bf16[128,2048]{1,0:T(8,128)(2,1)S(1)}, bf16[128,2048]{1,0:T(8,128)(2,1)}, u32[]{:S(2)}) copy-start(bf16[128,2048]{1,0:T(8,128)(2,1)} %param.17) | copy-start | bytes 1572868
  188.0 4.9 %copy-start.3 = (bf16[2048,1056]{1,0:T(8,128)(2,1)S(1)}, bf16[2048,1056]{1,0:T(8,128)(2,1)}, u32[]{:S(2)}) copy-start(bf16[2048,1056]{1,0:T(8,128)(2,1)} %all-gather.3.cloned.1.call-done) | copy-start | bytes 12976132
  200.8 34.0 %all-to-all-start.2 = ((bf16[64,18,256]{2,1,0:T(8,128)(2,1)}), bf16[64,18,256]{2,1,0:T(8,128)(2,1)S(1)}, u32[]{:S(2)}, u32[]{:S(2)}) async-start(bf16[64,18,256]{2,1,0:T(8,128)(2,1)} %pad_maximum_fusion.3), calls=%async_computation.3 | async-start | bytes 1572864 | tf_op jit(solution)/shard_map/all_to_all | solution.py:28
  213.4 41.8 %reduce-scatter.2.cloned.1.call-start = ((), (), s32[]{:S(2)}) async-start(), calls=%async_computation.6 | async-start | bytes 1179648 | tf_op jit(solution)/shard_map/reduce_scatter | solution.py:69
  216.2 1.4 copy-start.4
  240.8 13.5 %copy-start.8 = (s32[128,4]{0,1:T(4,128)S(1)}, s32[128,4]{0,1:T(4,128)}, u32[]{:S(2)}) copy-start(s32[128,4]{0,1:T(4,128)} %param.18) | copy-start | bytes 6148
  240.8 17.7 %copy-start.1 = (bf16[1,176,2048]{2,1,0:T(8,128)(2,1)S(1)}, bf16[1,176,2048]{2,1,0:T(8,128)(2,1)}, u32[]{:S(2)}) copy-start(bf16[1,176,2048]{2,1,0:T(8,128)(2,1)} %param.27) | copy-start | bytes 2162692
  242.4 11.6 %all-to-all-start.3 = ((f32[8,1,640]{2,1,0:T(1,128)}), f32[8,1,640]{2,1,0:T(1,128)S(1)}, u32[]{:S(2)}, u32[]{:S(2)}) async-start(f32[8,1,640]{2,1,0:T(1,128)} %broadcast_in_dim.23), calls=%async_computation.4 | async-start | bytes 40960 | tf_op jit(solution)/shard_map/all_to_all | solution.py:46
Sparse Core Ops, SparseCore 0:
  60.7 40.3 all-gather.4
  104.1 83.8 all-gather.2
  217.4 36.9 reduce-scatter.1
where the time goes:
time: 266 us; the launch traced here: 265 us
  waiting for transfers between devices  107 us (40%)
  local copies, waits for them, and re-layouts  40.2 us (15%)
  blocking collectives  38.9 us (15%)
  starting transfers between devices  24.9 us (9%)
  matrix products  21.4 us (8%)
  other arithmetic  18.6 us (7%)
  between operations  14.3 us (5%)
    all_gather x1, waiting for transfers between devices, turned_gather(): result, at, outs = (lax.all_gather(both, axis, axis=0, tiled=True), 0, [])  46.9 us
    all_gather x1, waiting for transfers between devices, in_one_piece_2(): lax.all_gather(both, axis, axis=dim, tiled=True)  39.5 us
    all_to_all x1, blocking collectives, in_one_piece(): lax.all_to_all(both, axis, split_axis=split_dim, concat_axis=concat_dim,...  38.9 us
    all_to_all x2, starting transfers between devices, in_one_piece(): lax.all_to_all(both, axis, split_axis=split_dim, concat_axis=concat_dim,...  17.7 us
    all_to_all x2, waiting for transfers between devices, in_one_piece(): lax.all_to_all(both, axis, split_axis=split_dim, concat_axis=concat_dim,...  16.9 us
    all_to_all x1, starting transfers between devices, copy_for_each(): lax.all_to_all(jnp.broadcast_to(x[None], (peers, *x.shape)), axis, 0, 0,...  6.92 us
    concatenate x3, other arithmetic, in_one_piece(): both = jnp.concatenate(arrays, axis=along)  5.99 us
    reshape x1, local copies, waits for them, and re-layouts, run_routed(): split_back = backward.reshape(buffer_rows, tensor_size, col_width)  5.82 us
  transfers between devices with their start and end apart: 6, of which 4 were waited for; matrix products, arithmetic and copies ran while one was open for 21% of the time, Pallas kernels for 0%

commit v1 on v0

v1 whole, which is shorter than its diff:
```python
import jax
import jax.numpy as jnp
from jax import lax
from jax.experimental import pallas as pl
from jax.experimental.pallas import tpu as pltpu
from jax.sharding import PartitionSpec as P

MESH = pl.DeviceIdType.MESH
F32 = jnp.float32
BF16 = jnp.bfloat16
RING = 8
XS = 4
CAP = 9
HALF = 32
TOK = 128
WIDTH = 2048
QUARTER = WIDTH // XS
EIGHTH = QUARTER // 2
PACK = 2 * QUARTER + 128
HID = 176
SHID = 352
SPAD = 384
MAIN = HALF * 8
ROWS = HALF * CAP


def mm(a, b):
    return jnp.dot(a, b, preferred_element_type=F32)


def nt(a, b):
    return lax.dot_general(a, b, (((1,), (1,)), ((), ())), preferred_element_type=F32)


def halves(v):
    high = v.astype(BF16)
    return high, (v - high.astype(F32)).astype(BF16)


def silu_pair(v):
    s = 1.0 / (1.0 + jnp.exp(-v))
    return v * s, s * (1.0 + v * (1.0 - s))


def iota(shape, dim):
    return lax.broadcasted_iota(jnp.int32, shape, dim)


def one_hot(mask):
    return jnp.where(mask, 1.0, 0.0).astype(BF16)


def unpack_into(rows_ref, blocks):
    flat = blocks.astype(F32).reshape(MAIN, PACK)
    rows_ref[0:MAIN, :] = flat[:, : 2 * QUARTER].astype(BF16)
    extra = flat[:, 2 * QUARTER :].astype(BF16)
    row, col = iota((HALF, MAIN), 0), iota((HALF, MAIN), 1)
    for q in range(8):
        ninth = mm(one_hot(col == row * 8 + q), extra)
        rows_ref[MAIN:ROWS, q * 128 : (q + 1) * 128] = ninth.astype(BF16)


def pack(main, ninth):
    sub = iota((MAIN, 128), 0) % 8
    extra = jnp.zeros((MAIN, 128), F32)
    for q in range(8):
        extra = jnp.where(sub == q, ninth[:, q * 128 : (q + 1) * 128], extra)
    return main.reshape(HALF, 8, 2 * QUARTER), extra.reshape(HALF, 8, 128)


def body(
    tok, cot, ids, emap, router, sgate, sh_own, wg_in, wu_in, wd_in,
    mixed_o, grad_o,
    send, gat, wg, wu, wd, xrow, acc, hid, gg, gu, outs, rs_a, rs_b, rs_l, rs_r,
    ret_s, ret_r, shw, sh_s, sh_r, px_s, px_r, dx_s, dx_r, sh_acc,
    local_sem, w_send, w_recv, d_send, d_recv, x_send, x_recv, rs_send, rs_recv,
    t_send, t_recv, p1_send, p1_recv, ra_send, ra_recv, la_send, la_recv,
    s_send, s_recv, px_sem, dx_send, dx_recv,
):
    dp = lax.axis_index("dp")
    tp = lax.axis_index("tensor")
    x, c = tp // 2, tp % 2
    mine = dp // 2
    parity = dp % 2
    peer_t = x * 2 + parity
    to_self = parity == c
    right = ((x + 1) % XS) * 2 + c
    left = ((x + XS - 1) % XS) * 2 + c
    opposite = ((x + 2) % XS) * 2 + c
    x1, x2, x3 = (x + 1) % XS, (x + 2) % XS, (x + 3) % XS
    zc, yc = dp // RING, dp % RING
    a_me = jnp.where(c == 0, yc, zc)
    b_me = jnp.where(c == 0, zc, yc)

    def line(a, b):
        return a * (1 + 7 * c) + b * (8 - 7 * c)

    def remote(src, dst, ssem, rsem, d, t):
        return pltpu.make_async_remote_copy(
            src_ref=src, dst_ref=dst, send_sem=ssem, recv_sem=rsem, device_id=(d, t), device_id_type=MESH
        )

    def drain(ref, sem):
        pltpu.make_async_copy(ref, ref, sem).wait()

    barrier = pltpu.get_barrier_semaphore()

    def greet(d, t):
        pl.semaphore_signal(barrier, inc=1, device_id=(d, t), device_id_type=MESH)

    def greet_peer(i, carry):
        d = 2 * i + c

        @pl.when(jnp.logical_not(jnp.logical_and(d == dp, to_self)))
        def _():
            greet(d, peer_t)

        return carry

    lax.fori_loop(0, HALF, greet_peer, 0)
    for off in range(1, 8):
        greet(dp, (tp + off) % 8)
        greet(line((a_me + off) % RING, b_me), tp)
    b_right = line(a_me, (b_me + 1) % RING)
    b_left = line(a_me, (b_me + 7) % RING)
    greet(b_right, tp)
    greet(b_left, tp)

    loads = [
        pltpu.make_async_copy(wg_in, wg.at[0], local_sem.at[0]),
        pltpu.make_async_copy(wu_in, wu.at[0], local_sem.at[1]),
        pltpu.make_async_copy(wd_in, wd.at[0], local_sem.at[2]),
        pltpu.make_async_copy(sh_own, shw.at[dp], local_sem.at[3]),
    ]
    for copy in loads:
        copy.start()

    place = iota((64, 64), 0)
    slot = 2 * (place % HALF) + place // HALF
    slot_map = jnp.where(slot == emap[...], 1.0, 0.0)
    slot_expert = slot_map.astype(BF16)
    expert = iota((64, TOK), 0)
    named = jnp.zeros((64, TOK), F32)
    for k in range(4):
        named = named + jnp.where(expert == ids[k : k + 1, :], 1.0, 0.0)
    chosen = mm(slot_expert, named.astype(BF16))
    before = one_hot(iota((TOK, TOK), 0) < iota((TOK, TOK), 1))
    rank1 = chosen * (mm(chosen.astype(BF16), before) + 1.0)
    rank1_b = rank1.astype(BF16)
    spread = one_hot(iota((MAIN, 64), 1) == c * HALF + iota((MAIN, 64), 0) // 8)
    wide = mm(spread, rank1_b)
    pick_main = one_hot(wide == (iota((MAIN, TOK), 0) % 8 + 1).astype(F32))
    pick_nine = one_hot(wide == float(CAP))
    quarter_cols = pl.ds(pl.multiple_of(x * QUARTER, 128), QUARTER)
    table = jnp.concatenate([tok[:, quarter_cols], cot[:, quarter_cols]], axis=1)
    block, extra = pack(mm(pick_main, table), mm(pick_nine, table))
    send[:, :, : 2 * QUARTER] = block.astype(BF16)
    send[:, :, 2 * QUARTER :] = extra.astype(BF16)

    pl.semaphore_wait(barrier, HALF + 16 - to_self.astype(jnp.int32))

    def a2a(src, dst, ssem, rsem):
        def step(n, carry):
            i = (mine + n) % HALF
            d = 2 * i + c
            own = jnp.logical_and(d == dp, to_self)

            @pl.when(own)
            def _():
                pltpu.make_async_copy(src.at[i], dst(mine), rsem).start()

            @pl.when(jnp.logical_not(own))
            def _():
                remote(src.at[i], dst(mine), ssem, rsem, d, peer_t).start()

            return carry

        lax.fori_loop(0, HALF, step, 0)

    def a2a_sent(src, ssem):
        @pl.when(to_self)
        def _():
            drain(src.at[0 : HALF - 1], ssem)

        @pl.when(jnp.logical_not(to_self))
        def _():
            drain(src, ssem)

    a2a(send, lambda i: gat.at[x, i], d_send, d_recv)

    w_copies = [
        remote(wg_in, wg.at[1], w_send.at[0], w_recv.at[0], dp, x * 2 + 1 - c),
        remote(wu_in, wu.at[1], w_send.at[1], w_recv.at[1], dp, x * 2 + 1 - c),
        remote(wd_in, wd.at[1], w_send.at[2], w_recv.at[2], dp, x * 2 + 1 - c),
    ]
    for copy in w_copies:
        copy.start()
    for off in range(1, 8):
        remote(sh_own, shw.at[dp], p1_send, p1_recv, line((a_me + off) % RING, b_me), tp).start()

    router_s = mm(slot_expert, router[...]).astype(BF16)
    logits = nt(router_s, tok[...])
    live = jnp.sum(slot_map, axis=1, keepdims=True) > 0.5
    expd = jnp.where(live, jnp.exp(logits), 0.0)
    prob = expd / jnp.sum(expd, axis=0, keepdims=True)
    gate_w = chosen * prob
    scale = 1.0 / (
        1.0 + jnp.exp(-jnp.sum(tok[...].astype(F32) * sgate[...].astype(F32), axis=1, keepdims=True))
    )

    drain(gat.at[x], d_recv)
    g0, g1 = slice(0, HALF // 2), slice(HALF // 2, HALF)

    def x_copy(n, q, g, t):
        return remote(gat.at[q, g], gat.at[q, g], x_send.at[n], x_recv.at[n], dp, t)

    first = [x_copy(0, x, g0, right), x_copy(1, x, g1, left), x_copy(2, x, g1, right), x_copy(3, x, g0, left)]
    for copy in first:
        copy.start()

    loads[3].wait()
    drain(shw.at[0:7], p1_recv)

    def line_send(b, lo, hi, ssem, rsem, target):
        for a in range(lo, hi):
            place_ = line(a, b % RING)
            remote(shw.at[place_], shw.at[place_], ssem, rsem, target, tp).start()

    def ring_step(k):
        if k > 1:
            drain(shw.at[0:8], ra_recv.at[k - 2])
            drain(shw.at[0:8], la_recv.at[k - 2])
        hi, lo = (8, 0) if k < 4 else (4, 4)
        line_send(b_me + RING - (k - 1), 0, hi, ra_send.at[k - 1], ra_recv.at[k - 1], b_right)
        line_send(b_me + (k - 1), lo, 8, la_send.at[k - 1], la_recv.at[k - 1], b_left)

    ring_step(1)
    for copy in loads[:3]:
        copy.wait()
    for copy in w_copies:
        copy.wait_recv()

    def feed(q, start):
        unpack_into(xrow, gat[q])
        at = pl.ds(pl.multiple_of(q * QUARTER, 128), QUARTER)
        for h in range(2):
            parts = (
                mm(xrow[:, :QUARTER], wg[h, at, :]),
                mm(xrow[:, :QUARTER], wu[h, at, :]),
                nt(xrow[:, QUARTER:], wd[h, :, at]),
            )
            for n, part in enumerate(parts):
                if start:
                    acc[3 * h + n] = part
                else:
                    acc[3 * h + n] += part

    feed(x, True)
    x_copy(0, x3, g0, left).wait_recv()
    ahead = x_copy(4, x3, g0, right)
    ahead.start()
    x_copy(1, x1, g1, right).wait_recv()
    back = x_copy(5, x1, g1, left)
    back.start()
    ring_step(2)
    x_copy(2, x3, g1, left).wait_recv()
    feed(x3, False)
    x_copy(3, x1, g0, right).wait_recv()
    feed(x1, False)
    ring_step(3)
    x_copy(4, x2, g0, left).wait_recv()
    x_copy(5, x2, g1, right).wait_recv()
    feed(x2, False)

    for h in range(2):
        active, slope = silu_pair(acc[3 * h])
        up, grad_hidden = acc[3 * h + 1], acc[3 * h + 2]
        hid[h] = (active * up).astype(BF16)
        gg[h] = (grad_hidden * up * slope).astype(BF16)
        gu[h] = (grad_hidden * active).astype(BF16)

    repeat = one_hot(iota((MAIN, HALF), 1) == iota((MAIN, HALF), 0) // 8)

    def produce(q):
        at = pl.ds(pl.multiple_of(q * QUARTER, 128), QUARTER)
        out = mm(hid[0], wd[0, :, at]) + mm(hid[1], wd[1, :, at])
        grad = nt(gg[0], wg[0, at, :]) + nt(gg[1], wg[1, at, :])
        grad = grad + nt(gu[0], wu[0, at, :]) + nt(gu[1], wu[1, at, :])
        both = jnp.concatenate([out, grad], axis=1)
        return pack(both[:MAIN], mm(repeat, both[MAIN:].astype(BF16)))

    def put(ref, packed):
        ref[:, :, : 2 * QUARTER] = packed[0].astype(BF16)
        ref[:, :, 2 * QUARTER :] = packed[1].astype(BF16)

    put(outs.at[0], produce(x2))
    rs_copies = [
        remote(outs.at[0, g0], rs_a, rs_send.at[0], rs_recv.at[0], dp, right),
        remote(outs.at[0, g1], rs_b, rs_send.at[1], rs_recv.at[1], dp, left),
        remote(outs.at[1], rs_l, rs_send.at[2], rs_recv.at[2], dp, right),
        remote(outs.at[2], rs_r, rs_send.at[3], rs_recv.at[3], dp, left),
    ]
    rs_copies[0].start()
    rs_copies[1].start()
    put(outs.at[1], produce(x1))
    put(outs.at[2], produce(x3))
    rs_copies[0].wait_recv()
    outs[1, g0] = (outs[1, g0].astype(F32) + rs_a[...].astype(F32)).astype(BF16)
    rs_copies[2].start()
    rs_copies[1].wait_recv()
    outs[2, g1] = (outs[2, g1].astype(F32) + rs_b[...].astype(F32)).astype(BF16)
    rs_copies[3].start()

    put(ret_s, produce(x))

    ring_step(4)
    drain(shw.at[0:4], ra_recv.at[3])
    drain(shw.at[0:4], la_recv.at[3])

    def shared_in(n, carry):
        cols = pl.ds(pl.multiple_of(n * QUARTER, 128), QUARTER)
        blocks = pl.ds(n * 16, 16)
        parts = (
            mm(tok[:, cols], shw[blocks, :, 0:SHID].reshape(QUARTER, SHID)),
            mm(tok[:, cols], shw[blocks, :, SPAD : SPAD + SHID].reshape(QUARTER, SHID)),
            mm(cot[:, cols], shw[blocks, :, 2 * SPAD : 2 * SPAD + SHID].reshape(QUARTER, SHID)),
        )
        for m, part in enumerate(parts):
            sh_acc[m] = part + jnp.where(n == 0, 0.0, 1.0) * sh_acc[m]
        return carry

    for m in range(3):
        sh_acc[m] = jnp.zeros((TOK, SHID), F32)
    lax.fori_loop(0, XS, shared_in, 0)
    active, slope = silu_pair(sh_acc[0])
    sh_grad = sh_acc[2]
    sh_hid = (active * sh_acc[1]).astype(BF16)
    sh_gg = (sh_grad * sh_acc[1] * slope).astype(BF16)
    sh_gu = (sh_grad * active).astype(BF16)
    dot_high, dot_low = halves(sh_hid.astype(F32) * sh_grad)
    ones_s = jnp.ones((8, SHID), BF16)
    dx_s[HALF : HALF + 8, :] = nt(ones_s, dot_high) + nt(ones_s, dot_low)

    def shared_out(q):
        blocks = pl.ds(q * 16, 16)
        out = nt(sh_hid, shw[blocks, :, 2 * SPAD : 2 * SPAD + SHID].reshape(QUARTER, SHID))
        grad = nt(sh_gg, shw[blocks, :, 0:SHID].reshape(QUARTER, SHID))
        grad = grad + nt(sh_gu, shw[blocks, :, SPAD : SPAD + SHID].reshape(QUARTER, SHID))
        return jnp.concatenate([out * scale, grad * scale], axis=1)

    rs_copies[2].wait_recv()
    rs_copies[3].wait_recv()
    ret_s[...] = (ret_s[...].astype(F32) + rs_l[...].astype(F32) + rs_r[...].astype(F32)).astype(BF16)
    a2a(ret_s, lambda i: ret_r.at[i], t_send, t_recv)

    sh_copies = []
    for n, (q, t) in enumerate(((x2, opposite), (x1, right), (x3, left))):
        sh_s[n] = shared_out(q).astype(BF16)
        copy = remote(sh_s.at[n], sh_r.at[n], s_send.at[n], s_recv.at[n], dp, t)
        copy.start()
        sh_copies.append(copy)
    total = shared_out(x)

    rank_t = rank1.T.astype(BF16)
    w_high, w_low = halves(gate_w.T)
    wide_t = nt(rank_t, spread)
    gate_t = nt(w_high, spread) + nt(w_low, spread)
    weigh_main = jnp.where(wide_t == (iota((TOK, MAIN), 1) % 8 + 1).astype(F32), gate_t, 0.0)
    spread9 = one_hot(iota((HALF, 64), 1) == c * HALF + iota((HALF, 64), 0))
    wide9_t = nt(rank_t, spread9)
    gate9_t = nt(w_high, spread9) + nt(w_low, spread9)
    weigh_nine = jnp.where(wide9_t == float(CAP), gate9_t, 0.0)
    main_high, main_low = halves(weigh_main)
    nine_high, nine_low = halves(weigh_nine)
    pick9 = one_hot(mm(spread9, rank1_b) == float(CAP))
    cot_main = mm(pick_main, table[:, QUARTER:])
    cot_nine = mm(pick9, table[:, QUARTER:])

    for copy in sh_copies:
        copy.wait_recv()

    total = total + sh_r[0].astype(F32) + sh_r[1].astype(F32) + sh_r[2].astype(F32)

    drain(ret_r, t_recv)
    unpack_into(xrow, ret_r[...])
    ones_q = jnp.ones((8, QUARTER), BF16)
    row_slot = iota((HALF, MAIN), 1) // 8 == iota((HALF, MAIN), 0)
    p_high, p_low = halves(cot_main * xrow[0:MAIN, :QUARTER].astype(F32))
    dots = nt(ones_q, p_high) + nt(ones_q, p_low)
    d_high, d_low = halves(jnp.where(row_slot, dots[0:1, :], 0.0))
    p_high, p_low = halves(cot_nine * xrow[MAIN:ROWS, :QUARTER].astype(F32))
    dots9 = nt(ones_q, p_high) + nt(ones_q, p_low)
    n_high, n_low = halves(jnp.where(iota((HALF, HALF), 0) == iota((HALF, HALF), 1), dots9[0:1, :], 0.0))
    dx_s[0:HALF, :] = mm(d_high, pick_main) + mm(d_low, pick_main) + mm(n_high, pick9) + mm(n_low, pick9)
    dx_r[tp] = dx_s[...]
    for off in range(1, 8):
        remote(dx_s, dx_r.at[tp], dx_send, dx_recv, dp, (tp + off) % 8).start()

    total = total + mm(main_high, xrow[0:MAIN, :]) + mm(main_low, xrow[0:MAIN, :])
    total = total + mm(nine_high, xrow[MAIN:ROWS, :]) + mm(nine_low, xrow[MAIN:ROWS, :])
    low = jnp.concatenate([total[:, 0:EIGHTH], total[:, QUARTER : QUARTER + EIGHTH]], axis=1)
    high = jnp.concatenate([total[:, EIGHTH:QUARTER], total[:, QUARTER + EIGHTH :]], axis=1)
    px_s[...] = jnp.where(c == 0, high, low)
    own = jnp.where(c == 0, low, high)
    px = remote(px_s, px_r, px_sem.at[0], px_sem.at[1], dp, x * 2 + 1 - c)
    px.start()

    drain(dx_r.at[0:7], dx_recv)
    even = dx_r[0] + dx_r[2] + dx_r[4] + dx_r[6]
    odd = dx_r[1] + dx_r[3] + dx_r[5] + dx_r[7]
    slot_dots = jnp.concatenate([even[0:HALF], odd[0:HALF]], axis=0)
    sh_dots = (even[HALF : HALF + 8] + odd[HALF : HALF + 8]).T[:, 0:1]
    taken = chosen * slot_dots
    dlogits = prob * (taken - jnp.sum(gate_w * slot_dots, axis=0, keepdims=True))
    l_high, l_low = halves(dlogits.T)
    router_q = mm(slot_expert, router[:, pl.ds(pl.multiple_of(tp * EIGHTH, 128), EIGHTH)]).astype(BF16)
    grad = mm(l_high, router_q) + mm(l_low, router_q)
    sg_cols = sgate[:, pl.ds(pl.multiple_of(tp * EIGHTH, 128), EIGHTH)].astype(F32)
    grad = grad + sh_dots * scale * (1.0 - scale) * sg_cols
    px.wait_recv()
    both = own + px_r[...]
    mixed_o[...] = both[:, :EIGHTH].astype(BF16)
    grad_o[...] = (both[:, EIGHTH:] + grad).astype(BF16)

    a2a_sent(send, d_send)
    a2a_sent(ret_s, t_send)
    for copy in (*w_copies, *first, ahead, back, *rs_copies, *sh_copies, px):
        copy.wait_send()
    drain(shw.at[0:7], p1_send)
    for k in range(4):
        count = 8 if k < 3 else 4
        drain(shw.at[0:count], ra_send.at[k])
        drain(shw.at[0:count], la_send.at[k])
    drain(dx_r.at[0:7], dx_send)


def shards(
    tokens, grad_out, route_ids, expert_map, router, shared_gate, sh_gate, sh_up, sh_down, ex_gate, ex_up, ex_down
):
    ids = jnp.pad(route_ids.T, ((0, 4), (0, 0)), constant_values=-1)
    emap = jnp.pad(expert_map, (0, 4), constant_values=-1).reshape(1, 64)
    router_t = jnp.pad(router.T, ((0, 4), (0, 0)))
    own = jnp.concatenate([jnp.pad(a, ((0, 0), (0, SPAD - SHID))) for a in (sh_gate, sh_up, sh_down.T)], axis=1)
    vmem = pl.BlockSpec(memory_space=pltpu.VMEM)
    hbm = pl.BlockSpec(memory_space=pl.ANY)
    dma = pltpu.SemaphoreType.DMA
    block = (HALF, 8, PACK)
    return pl.pallas_call(
        body,
        out_shape=(jax.ShapeDtypeStruct((TOK, EIGHTH), BF16), jax.ShapeDtypeStruct((TOK, EIGHTH), BF16)),
        in_specs=[vmem] * 7 + [hbm] * 3,
        out_specs=(vmem, vmem),
        scratch_shapes=[
            pltpu.VMEM(block, BF16),
            pltpu.VMEM((XS, *block), BF16),
            pltpu.VMEM((2, WIDTH, HID), BF16),
            pltpu.VMEM((2, WIDTH, HID), BF16),
            pltpu.VMEM((2, HID, WIDTH), BF16),
            pltpu.VMEM((ROWS, 2 * QUARTER), BF16),
            pltpu.VMEM((6, ROWS, HID), F32),
            pltpu.VMEM((2, ROWS, HID), BF16),
            pltpu.VMEM((2, ROWS, HID), BF16),
            pltpu.VMEM((2, ROWS, HID), BF16),
            pltpu.VMEM((3, *block), BF16),
            pltpu.VMEM((HALF // 2, 8, PACK), BF16),
            pltpu.VMEM((HALF // 2, 8, PACK), BF16),
            pltpu.VMEM(block, BF16),
            pltpu.VMEM(block, BF16),
            pltpu.VMEM(block, BF16),
            pltpu.VMEM(block, BF16),
            pltpu.VMEM((RING * RING, 32, 3 * SPAD), BF16),
            pltpu.VMEM((3, TOK, 2 * QUARTER), BF16),
            pltpu.VMEM((3, TOK, 2 * QUARTER), BF16),
            pltpu.VMEM((TOK, QUARTER), F32),
            pltpu.VMEM((TOK, QUARTER), F32),
            pltpu.VMEM((HALF + 8, TOK), F32),
            pltpu.VMEM((8, HALF + 8, TOK), F32),
            pltpu.VMEM((3, TOK, SHID), F32),
            dma((4,)), dma((3,)), dma((3,)), dma, dma, dma((6,)), dma((6,)), dma((4,)), dma((4,)),
            dma, dma, dma, dma, dma((4,)), dma((4,)), dma((4,)), dma((4,)),
            dma((3,)), dma((3,)), dma((2,)), dma, dma,
        ],
        compiler_params=pltpu.CompilerParams(
            collective_id=0, has_side_effects=True, vmem_limit_bytes=60 * 1024 * 1024
        ),
    )(
        tokens, grad_out, ids, emap, router_t, shared_gate.reshape(1, WIDTH), own,
        ex_gate.reshape(WIDTH, HID), ex_up.reshape(WIDTH, HID), ex_down.reshape(HID, WIDTH),
    )


def solution(mesh):
    placed = (
        P("dp", None), P("dp", None), P("dp", None), P(), P(), P(),
        P("dp", "tensor"), P("dp", "tensor"), P("tensor", "dp"),
        P("dp", None, "tensor"), P("dp", None, "tensor"), P("dp", "tensor", None),
    )
    return jax.shard_map(
        shards,
        mesh=mesh,
        in_specs=placed,
        out_specs=(P("dp", "tensor"), P("dp", "tensor")),
        check_vma=False,
    )
```

time: 266 us -> 128 us (0.48)
  Pallas kernels: 0 us -> 115 us
  waiting for transfers between devices: 107 us -> 0 us
  blocking collectives: 38.9 us -> 0 us
  local copies, waits for them, and re-layouts: 40.2 us -> 11.2 us
  starting transfers between devices: 24.9 us -> 0 us
  matrix products: 21.4 us -> 0 us
  other arithmetic: 18.6 us -> 1.4 us
  between operations: 14.3 us -> 0.66 us
    pallas_call x0 -> x1, Pallas kernels: none -> 115 us  [shards(): pl.pallas_call(body, out_shape=(jax.ShapeDtypeStruct((TOK, EIGHTH), BF16)...]
    all_gather x2 -> x0, waiting for transfers between devices: 86.4 us -> none  [the longest x1 46.9 us: turned_gather(): result, at, outs = (lax.all_gather(both, axis, axis=0, tiled=True), 0, [])]
    all_to_all x1 -> x0, blocking collectives: 38.9 us -> none  [in_one_piece(): lax.all_to_all(both, axis, split_axis=split_dim, concat_axis=concat_dim,...]
    all_to_all x3 -> x0, starting transfers between devices: 24.6 us -> none  [the longest x2 17.7 us: in_one_piece(): lax.all_to_all(both, axis, split_axis=split_dim, concat_axis=concat_dim,...]
    dot_general x14 -> x0, matrix products: 21.4 us -> none  [the longest x3 2.78 us: contract_last(): lax.dot_general(left, right, (((1,), (1,)), ((), ())), preferred_element_...]
    all_to_all x3 -> x0, waiting for transfers between devices: 20.2 us -> none  [the longest x2 16.9 us: in_one_piece(): lax.all_to_all(both, axis, split_axis=split_dim, concat_axis=concat_dim,...]
    reshape x8 -> x2, local copies, waits for them, and re-layouts: 13.3 us -> 2.53 us  [the longest x1 1.29 us: shards(): shared_gate.reshape(1, WIDTH)]
    gather x4 -> x0, local copies, waits for them, and re-layouts: 8.61 us -> none  [the longest x2 5.46 us: fetch_rows(): return jnp.take(padded, source_rows, axis=0)]
  transfers between devices with their start and end apart: 6 -> 0, of which waited for: 4 -> 0; matrix products, arithmetic and copies ran while one was open for 21% -> 0% of each run, Pallas kernels for 0% -> 0%
where the time goes in v1:
time: 128 us
  Pallas kernels  115 us (90%)
  local copies, waits for them, and re-layouts  11.2 us (9%)
  other arithmetic  1.4 us (1%)
    pallas_call x1, Pallas kernels, shards(): pl.pallas_call(body, out_shape=(jax.ShapeDtypeStruct((TOK, EIGHTH), BF16)...  115 us
    unnamed x10, local copies, waits for them, and re-layouts  5.69 us

profile of v1, /device:TPU:1, one launch (start us, length us, event | category | flops | bytes accessed | tf_op | source)
XLA Modules:
  0.0 127.8 jit_solution(3991809233554904755)
XLA Ops:
  0.6 0.0 copy-start.2
  0.6 1.2 pad_bitcast_fusion.emap
  1.9 1.3 pad.22.ids
  3.2 1.3 %reshape.20.sgate = bf16[1,2048]{1,0:T(2,128)(2,1)} reshape(bf16[2048]{0:T(1024)(128)(2,1)} %param.17) | data formatting | bytes 8192 | tf_op jit(solution)/shard_map/reshape | solution.py:487
  4.4 0.0 copy-done.2
  4.5 1.4 %fusion.5.sh_own = bf16[32,1152]{1,0:T(8,128)(2,1)} fusion(bf16[32,352]{1,0:T(8,128)(2,1)S(1)} %bitcast.12, bf16[32,352]{1,0:T(8,128)(2,1)} %param.19, bf16[32,352]{1,0:T(8,128)(2,1)} %param.18), kind=kLoop, calls=%fused_computation.9 | loop fusion | flops 516096 | bytes 141312 | tf_op jit(solution)/shard_map/concatenate | solution.py:443
  5.8 1.7 %pad.24.router = bf16[64,2048]{1,0:T(8,128)(2,1)} pad(bf16[60,2048]{1,0:T(8,128)(2,1)} %bitcast.11, bf16[]{:T(256)} %constant.4.clone.1), padding=0_4x0_0 | pad | bytes 507906 | tf_op jit(solution)/shard_map/jit(_pad)/pad | solution.py:442
  7.5 0.0 copy-start
  7.5 2.3 %copy.14 = bf16[1,2048,176]{2,1,0:T(8,128)(2,1)} copy(bf16[1,2048,176]{1,2,0:T(8,128)(2,1)} %param.21) | data formatting | bytes 1441792 | tf_op args[9]
  9.8 0.0 copy-done
  9.8 1.3 %copy.15 = bf16[1,2048,176]{2,1,0:T(8,128)(2,1)} copy(bf16[1,2048,176]{1,2,0:T(8,128)(2,1)S(1)} %copy-done) | data formatting | bytes 1441792 | tf_op args[10]
  11.1 114.6 %shard_map.131 = (bf16[128,256]{1,0:T(8,128)(2,1)}, bf16[128,256]{1,0:T(8,128)(2,1)}) custom-call(bf16[128,2048]{1,0:T(8,128)(2,1)} %tok.1, bf16[128,2048]{1,0:T(8,128)(2,1)} %cot.1, s32[8,128]{1,0:T(8,128)} %pad.22.ids, s32[1,64]{1,0:T(1,128)} %pad_bitcast_fusion.emap, bf16[64,2048]{1,0:T(8,128)(2,1)} %pad.24.router, bf16[1,2048]{1,0:T(2,128)(2,1)} %reshape.20.sgate, ...), custom_call_target="tpu_custom_call" | custom-call | tf_op jit(solution)/shard_map/pallas_call | solution.py:448
  125.7 0.0 copy-start.1
  125.7 1.5 %copy.18 = bf16[128,256]{1,0:T(8,128)(2,1)} copy(bf16[128,256]{1,0:T(8,128)(2,1)} %get-tuple-element.4) | data formatting | bytes 131072
  127.2 0.0 copy-done.1
  127.2 0.6 copy.19
Async XLA Ops:
  0.6 3.8 %copy-start.2 = (bf16[352,32]{0,1:T(8,128)(2,1)S(1)}, bf16[352,32]{0,1:T(8,128)(2,1)}, u32[]{:S(2)}) copy-start(bf16[352,32]{0,1:T(8,128)(2,1)} %param.20) | copy-start | bytes 67588
  7.5 2.3 %copy-start = (bf16[1,2048,176]{1,2,0:T(8,128)(2,1)S(1)}, bf16[1,2048,176]{1,2,0:T(8,128)(2,1)}, u32[]{:S(2)}) copy-start(bf16[1,2048,176]{1,2,0:T(8,128)(2,1)} %param.22) | copy-start | bytes 2162692
  125.7 1.5 %copy-start.1 = (bf16[128,256]{1,0:T(8,128)(2,1)S(1)}, bf16[128,256]{1,0:T(8,128)(2,1)}, u32[]{:S(2)}) copy-start(bf16[128,256]{1,0:T(8,128)(2,1)} %get-tuple-element.5) | copy-start | bytes 196612

commit v2 on v1

v2 whole, which is shorter than its diff:
```python
import jax
import jax.numpy as jnp
from jax import lax
from jax.experimental import pallas as pl
from jax.experimental.pallas import tpu as pltpu
from jax.sharding import PartitionSpec as P

MESH = pl.DeviceIdType.MESH
F32 = jnp.float32
BF16 = jnp.bfloat16
RING = 8
XS = 4
CAP = 9
HALF = 32
TOK = 128
WIDTH = 2048
QUARTER = WIDTH // XS
EIGHTH = QUARTER // 2
PACK = 2 * QUARTER + 128
HID = 176
SHID = 352
SPAD = 384
MAIN = HALF * 8
ROWS = HALF * CAP


def mm(a, b):
    return jnp.dot(a, b, preferred_element_type=F32)


def nt(a, b):
    return lax.dot_general(a, b, (((1,), (1,)), ((), ())), preferred_element_type=F32)


def halves(v):
    high = v.astype(BF16)
    return high, (v - high.astype(F32)).astype(BF16)


def silu_pair(v):
    s = 1.0 / (1.0 + jnp.exp(-v))
    return v * s, s * (1.0 + v * (1.0 - s))


def iota(shape, dim):
    return lax.broadcasted_iota(jnp.int32, shape, dim)


def one_hot(mask):
    return jnp.where(mask, 1.0, 0.0).astype(BF16)


def unpack_into(rows_ref, blocks):
    flat = blocks.astype(F32).reshape(MAIN, PACK)
    rows_ref[0:MAIN, :] = flat[:, : 2 * QUARTER].astype(BF16)
    extra = flat[:, 2 * QUARTER :].astype(BF16)
    row, col = iota((HALF, MAIN), 0), iota((HALF, MAIN), 1)
    for q in range(8):
        ninth = mm(one_hot(col == row * 8 + q), extra)
        rows_ref[MAIN:ROWS, q * 128 : (q + 1) * 128] = ninth.astype(BF16)


def pack(main, ninth):
    sub = iota((MAIN, 128), 0) % 8
    extra = jnp.zeros((MAIN, 128), F32)
    for q in range(8):
        extra = jnp.where(sub == q, ninth[:, q * 128 : (q + 1) * 128], extra)
    return main.reshape(HALF, 8, 2 * QUARTER), extra.reshape(HALF, 8, 128)


def body(
    tok, cot, ids, emap, router, sgate_in, sh_gate, sh_up, sh_down, wg_in, wu_in, wd_in,
    mixed_o, grad_o,
    send, gat, wg, wu, wd, xrow, acc, hid, gg, gu, outs, rs_a, rs_b, rs_l, rs_r,
    ret_s, ret_r, shw, sh_own, sgate, sh_s, sh_r, px_s, px_r, dx_s, dx_r, sh_acc, dot_s, dot_r,
    local_sem, w_send, w_recv, d_send, d_recv, x_send, x_recv, rs_send, rs_recv,
    t_send, t_recv, p1_send, p1_recv, ra_send, ra_recv, la_send, la_recv,
    s_send, s_recv, px_sem, dx_send, dx_recv, o_send, o_recv,
):
    dp = lax.axis_index("dp")
    tp = lax.axis_index("tensor")
    x, c = tp // 2, tp % 2
    mine = dp // 2
    parity = dp % 2
    peer_t = x * 2 + parity
    to_self = parity == c
    right = ((x + 1) % XS) * 2 + c
    left = ((x + XS - 1) % XS) * 2 + c
    opposite = ((x + 2) % XS) * 2 + c
    x1, x2, x3 = (x + 1) % XS, (x + 2) % XS, (x + 3) % XS
    zc, yc = dp // RING, dp % RING
    a_me = jnp.where(c == 0, yc, zc)
    b_me = jnp.where(c == 0, zc, yc)

    def line(a, b):
        return a * (1 + 7 * c) + b * (8 - 7 * c)

    def offset(k):
        return jnp.where(k % 2 == 0, k // 2, HALF - (k + 1) // 2)

    def peer_of(k):
        return (mine + offset(k)) % HALF

    def remote(src, dst, ssem, rsem, d, t):
        return pltpu.make_async_remote_copy(
            src_ref=src, dst_ref=dst, send_sem=ssem, recv_sem=rsem, device_id=(d, t), device_id_type=MESH
        )

    def drain(ref, sem):
        pltpu.make_async_copy(ref, ref, sem).wait()

    barrier = pltpu.get_barrier_semaphore()

    def greet(d, t):
        pl.semaphore_signal(barrier, inc=1, device_id=(d, t), device_id_type=MESH)

    def greet_peer(i, carry):
        d = 2 * i + c

        @pl.when(jnp.logical_not(jnp.logical_and(d == dp, to_self)))
        def _():
            greet(d, peer_t)

        return carry

    lax.fori_loop(0, HALF, greet_peer, 0)
    for off in range(1, 8):
        greet(dp, (tp + off) % 8)
        greet(line((a_me + off) % RING, b_me), tp)
    b_right = line(a_me, (b_me + 1) % RING)
    b_left = line(a_me, (b_me + 7) % RING)
    greet(b_right, tp)
    greet(b_left, tp)

    loads = [
        pltpu.make_async_copy(wg_in, wg.at[0], local_sem.at[0]),
        pltpu.make_async_copy(wu_in, wu.at[0], local_sem.at[1]),
        pltpu.make_async_copy(wd_in, wd.at[0], local_sem.at[2]),
        pltpu.make_async_copy(sh_own, shw.at[dp], local_sem.at[3]),
    ]
    for copy in loads[:3]:
        copy.start()
    for n, piece in enumerate((sh_gate, sh_up, sh_down)):
        sh_own[:, n * SPAD : n * SPAD + SHID] = piece[...]
        sh_own[:, n * SPAD + SHID : (n + 1) * SPAD] = jnp.zeros((32, SPAD - SHID), BF16)
    for n in range(WIDTH // 128):
        sgate[:, n * 128 : (n + 1) * 128] = sgate_in[n : n + 1, :].astype(F32)

    place = iota((64, 60), 0)
    slot = 2 * (place % HALF) + place // HALF
    slot_map = jnp.where(slot == emap[...], 1.0, 0.0)
    slot_expert = slot_map.astype(BF16)
    expert = iota((60, TOK), 0)
    named = jnp.zeros((60, TOK), F32)
    for k in range(4):
        named = named + jnp.where(expert == ids[k : k + 1, :], 1.0, 0.0)
    chosen = mm(slot_expert, named.astype(BF16))
    before = one_hot(iota((TOK, TOK), 0) < iota((TOK, TOK), 1))
    rank1 = chosen * (mm(chosen.astype(BF16), before) + 1.0)
    rank1_b = rank1.astype(BF16)
    spread = one_hot(iota((MAIN, 64), 1) == c * HALF + peer_of(iota((MAIN, 64), 0) // 8))
    wide = mm(spread, rank1_b)
    pick_main = one_hot(wide == (iota((MAIN, TOK), 0) % 8 + 1).astype(F32))
    pick_nine = one_hot(wide == float(CAP))
    quarter_cols = pl.ds(pl.multiple_of(x * QUARTER, 128), QUARTER)
    table = jnp.concatenate([tok[:, quarter_cols], cot[:, quarter_cols]], axis=1)
    block, extra = pack(mm(pick_main, table), mm(pick_nine, table))
    send[:, :, : 2 * QUARTER] = block.astype(BF16)
    send[:, :, 2 * QUARTER :] = extra.astype(BF16)

    pl.semaphore_wait(barrier, HALF + 16 - to_self.astype(jnp.int32))

    def a2a(src, dst, ssem, rsem, lo, hi, sign):
        def step(k, carry):
            i = (mine + sign * offset(k) + HALF) % HALF
            own = jnp.logical_and(k == 0, to_self)

            @pl.when(own)
            def _():
                pltpu.make_async_copy(src.at[k], dst(k), rsem).start()

            @pl.when(jnp.logical_not(own))
            def _():
                remote(src.at[k], dst(k), ssem, rsem, 2 * i + c, peer_t).start()

            return carry

        lax.fori_loop(lo, hi, step, 0)

    def a2a_sent(src, ssem):
        @pl.when(to_self)
        def _():
            drain(src.at[0 : HALF - 1], ssem)

        @pl.when(jnp.logical_not(to_self))
        def _():
            drain(src, ssem)

    a2a(send, lambda k: gat.at[x, k], d_send, d_recv.at[0], 0, 16, 1)
    a2a(send, lambda k: gat.at[x, k], d_send, d_recv.at[1], 16, HALF, 1)

    loads[3].start()

    w_copies = [
        remote(wg_in, wg.at[1], w_send.at[0], w_recv.at[0], dp, x * 2 + 1 - c),
        remote(wu_in, wu.at[1], w_send.at[1], w_recv.at[1], dp, x * 2 + 1 - c),
        remote(wd_in, wd.at[1], w_send.at[2], w_recv.at[2], dp, x * 2 + 1 - c),
    ]
    for copy in w_copies:
        copy.start()
    for off in range(1, 8):
        remote(sh_own, shw.at[dp], p1_send, p1_recv, line((a_me + off) % RING, b_me), tp).start()

    router_s = mm(slot_expert, router[...]).astype(BF16)
    logits = nt(router_s, tok[...])
    live = jnp.sum(slot_map, axis=1, keepdims=True) > 0.5
    expd = jnp.where(live, jnp.exp(logits), 0.0)
    prob = expd / jnp.sum(expd, axis=0, keepdims=True)
    gate_w = chosen * prob
    scale = 1.0 / (
        1.0 + jnp.exp(-jnp.sum(tok[...].astype(F32) * sgate[...], axis=1, keepdims=True))
    )

    h = [slice(8 * n, 8 * n + 8) for n in range(4)]

    def x_copy(n, q, part, t):
        return remote(gat.at[q, part], gat.at[q, part], x_send.at[n], x_recv.at[n], dp, t)

    sent = []

    def go(copy):
        copy.start()
        sent.append(copy)

    def x_first(n, part, other):
        drain(gat.at[x, 0:16], d_recv.at[n // 6])
        go(x_copy(n, x, part, right))
        go(x_copy(n + 1, x, other, left))
        go(x_copy(n + 2, x, other, right))
        go(x_copy(n + 3, x, part, left))

    def x_forward(n, part, other):
        x_copy(n, x3, part, left).wait_recv()
        go(x_copy(n + 4, x3, part, right))
        x_copy(n + 1, x1, other, right).wait_recv()
        go(x_copy(n + 5, x1, other, left))

    x_first(0, h[0], h[1])
    x_forward(0, h[0], h[1])
    x_first(6, h[2], h[3])

    loads[3].wait()
    drain(shw.at[0:7], p1_recv)

    def line_send(b, half, ssem, rsem, target):
        for a in range(4 * half, 4 * half + 4):
            at_ = line(a, b % RING)
            remote(shw.at[at_], shw.at[at_], ssem, rsem, target, tp).start()

    def ring_step(k, half):
        n = 2 * (k - 1) + half
        if k > 1:
            drain(shw.at[0:4], ra_recv.at[n - 2])
            drain(shw.at[0:4], la_recv.at[n - 2])
        if k < 4 or half == 0:
            line_send(b_me + RING - (k - 1), half, ra_send.at[n], ra_recv.at[n], b_right)
        if k < 4 or half == 1:
            line_send(b_me + (k - 1), half, la_send.at[n], la_recv.at[n], b_left)

    ring_step(1, 0)
    ring_step(1, 1)
    for copy in loads[:3]:
        copy.wait()
    for copy in w_copies:
        copy.wait_recv()

    def feed(q, start):
        unpack_into(xrow, gat[q])
        at = pl.ds(pl.multiple_of(q * QUARTER, 128), QUARTER)
        for p in range(2):
            parts = (
                nt(xrow[:, :QUARTER], wg[p, :, at]),
                nt(xrow[:, :QUARTER], wu[p, :, at]),
                nt(xrow[:, QUARTER:], wd[p, :, at]),
            )
            for n, part in enumerate(parts):
                if start:
                    acc[3 * p + n] = part
                else:
                    acc[3 * p + n] += part

    x_copy(2, x3, h[1], left).wait_recv()
    x_copy(3, x1, h[0], right).wait_recv()
    x_copy(4, x2, h[0], left).wait_recv()
    x_copy(5, x2, h[1], right).wait_recv()
    feed(x, True)
    x_forward(6, h[2], h[3])
    ring_step(2, 0)
    ring_step(2, 1)
    x_copy(8, x3, h[3], left).wait_recv()
    feed(x3, False)
    x_copy(9, x1, h[2], right).wait_recv()
    feed(x1, False)
    x_copy(10, x2, h[2], left).wait_recv()
    x_copy(11, x2, h[3], right).wait_recv()
    feed(x2, False)

    row_dots = jnp.zeros((ROWS, 1), F32)
    for p in range(2):
        active, slope = silu_pair(acc[3 * p])
        up, grad_hidden = acc[3 * p + 1], acc[3 * p + 2]
        hid[p] = (active * up).astype(BF16)
        gg[p] = (grad_hidden * up * slope).astype(BF16)
        gu[p] = (grad_hidden * active).astype(BF16)
        row_dots = row_dots + jnp.sum(hid[p].astype(F32) * grad_hidden, axis=1, keepdims=True)

    repeat = one_hot(iota((MAIN, HALF), 1) == iota((MAIN, HALF), 0) // 8)

    def produce(q):
        at = pl.ds(pl.multiple_of(q * QUARTER, 128), QUARTER)
        out = mm(hid[0], wd[0, :, at]) + mm(hid[1], wd[1, :, at])
        grad = mm(gg[0], wg[0, :, at]) + mm(gg[1], wg[1, :, at])
        grad = grad + mm(gu[0], wu[0, :, at]) + mm(gu[1], wu[1, :, at])
        both = jnp.concatenate([out, grad], axis=1)
        return pack(both[:MAIN], mm(repeat, both[MAIN:].astype(BF16)))

    def put(ref, packed):
        ref[:, :, : 2 * QUARTER] = packed[0].astype(BF16)
        ref[:, :, 2 * QUARTER :] = packed[1].astype(BF16)

    def rs_copy(n, src, dst, t):
        return remote(src, dst, rs_send.at[n], rs_recv.at[n], dp, t)

    def add_part(ref, at, more):
        ref[at] = (ref[at].astype(F32) + more.astype(F32)).astype(BF16)

    put(outs.at[0], produce(x2))
    go(rs_copy(0, outs.at[0, h[2]], rs_a.at[0], right))
    go(rs_copy(1, outs.at[0, h[3]], rs_b.at[0], left))
    put(outs.at[1], produce(x1))
    go(rs_copy(2, outs.at[1, h[3]], rs_l.at[h[3]], right))
    put(outs.at[2], produce(x3))
    go(rs_copy(3, outs.at[2, h[2]], rs_r.at[h[2]], left))

    n_high, n_low = halves(jnp.broadcast_to(row_dots[MAIN:], (HALF, 128)))
    ninth_dots = mm(repeat, n_high) + mm(repeat, n_low)
    both_dots = jnp.where(iota((MAIN, 128), 1) < 64, jnp.broadcast_to(row_dots[:MAIN], (MAIN, 128)), ninth_dots)
    dot_s[...] = both_dots.reshape(HALF, 8, 128)

    put(ret_s, produce(x))
    a2a(dot_s, lambda k: dot_r.at[k], o_send, o_recv, 0, HALF, -1)
    ring_step(3, 0)
    rs_copy(0, outs.at[0, h[2]], rs_a.at[0], left).wait_recv()
    add_part(outs, (1, h[2]), rs_a[0])
    go(rs_copy(4, outs.at[1, h[2]], rs_l.at[h[2]], right))
    rs_copy(1, outs.at[0, h[3]], rs_b.at[0], right).wait_recv()
    add_part(outs, (2, h[3]), rs_b[0])
    go(rs_copy(5, outs.at[2, h[3]], rs_r.at[h[3]], left))
    go(rs_copy(6, outs.at[0, h[0]], rs_a.at[1], right))
    go(rs_copy(7, outs.at[0, h[1]], rs_b.at[1], left))
    go(rs_copy(8, outs.at[1, h[1]], rs_l.at[h[1]], right))
    go(rs_copy(9, outs.at[2, h[0]], rs_r.at[h[0]], left))
    ring_step(3, 1)
    ring_step(4, 0)

    far, near = slice(16, HALF), slice(0, 16)
    for n, part in ((2, h[3]), (4, h[2])):
        rs_copy(n, outs.at[1, part], rs_l.at[part], left).wait_recv()
    for n, part in ((3, h[2]), (5, h[3])):
        rs_copy(n, outs.at[2, part], rs_r.at[part], right).wait_recv()
    add_part(ret_s, far, rs_l[far].astype(F32) + rs_r[far].astype(F32))
    a2a(ret_s, lambda k: ret_r.at[k], t_send, t_recv.at[1], 16, HALF, -1)
    ring_step(4, 1)

    drain(shw.at[0:4], ra_recv.at[6])
    drain(shw.at[0:4], la_recv.at[7])

    def shared_in(n, carry):
        cols = pl.ds(pl.multiple_of(n * QUARTER, 128), QUARTER)
        blocks = pl.ds(n * 16, 16)
        parts = (
            mm(tok[:, cols], shw[blocks, :, 0:SHID].reshape(QUARTER, SHID)),
            mm(tok[:, cols], shw[blocks, :, SPAD : SPAD + SHID].reshape(QUARTER, SHID)),
            mm(cot[:, cols], shw[blocks, :, 2 * SPAD : 2 * SPAD + SHID].reshape(QUARTER, SHID)),
        )
        for m, part in enumerate(parts):
            sh_acc[m] = part + jnp.where(n == 0, 0.0, 1.0) * sh_acc[m]
        return carry

    rs_copy(6, outs.at[0, h[0]], rs_a.at[1], left).wait_recv()
    add_part(outs, (1, h[0]), rs_a[1])
    go(rs_copy(10, outs.at[1, h[0]], rs_l.at[h[0]], right))
    rs_copy(7, outs.at[0, h[1]], rs_b.at[1], right).wait_recv()
    add_part(outs, (2, h[1]), rs_b[1])
    go(rs_copy(11, outs.at[2, h[1]], rs_r.at[h[1]], left))

    for m in range(3):
        sh_acc[m] = jnp.zeros((TOK, SHID), F32)
    lax.fori_loop(0, XS, shared_in, 0)
    active, slope = silu_pair(sh_acc[0])
    sh_grad = sh_acc[2]
    sh_hid = (active * sh_acc[1]).astype(BF16)
    sh_gg = (sh_grad * sh_acc[1] * slope).astype(BF16)
    sh_gu = (sh_grad * active).astype(BF16)
    dot_high, dot_low = halves(sh_hid.astype(F32) * sh_grad)
    ones_s = jnp.ones((8, SHID), BF16)
    dx_s[HALF : HALF + 8, :] = nt(ones_s, dot_high) + nt(ones_s, dot_low)

    def shared_out(q):
        blocks = pl.ds(q * 16, 16)
        out = nt(sh_hid, shw[blocks, :, 2 * SPAD : 2 * SPAD + SHID].reshape(QUARTER, SHID))
        grad = nt(sh_gg, shw[blocks, :, 0:SHID].reshape(QUARTER, SHID))
        grad = grad + nt(sh_gu, shw[blocks, :, SPAD : SPAD + SHID].reshape(QUARTER, SHID))
        return jnp.concatenate([out * scale, grad * scale], axis=1)

    def s_copy(n, src, dst, t):
        return remote(src, dst, s_send.at[n], s_recv.at[n], dp, t)

    top, low_ = slice(0, 64), slice(64, TOK)
    sh_s[0] = shared_out(x2).astype(BF16)
    go(s_copy(0, sh_s.at[0, top], sh_r.at[0, top], right))
    go(s_copy(1, sh_s.at[0, low_], sh_r.at[0, low_], left))
    sh_s[1] = shared_out(x1).astype(BF16)
    go(s_copy(2, sh_s.at[1, low_], sh_r.at[1, low_], right))
    sh_s[2] = shared_out(x3).astype(BF16)
    go(s_copy(3, sh_s.at[2, top], sh_r.at[2, top], left))

    for n, part in ((8, h[1]), (10, h[0])):
        rs_copy(n, outs.at[1, part], rs_l.at[part], left).wait_recv()
    for n, part in ((9, h[0]), (11, h[1])):
        rs_copy(n, outs.at[2, part], rs_r.at[part], right).wait_recv()
    add_part(ret_s, near, rs_l[near].astype(F32) + rs_r[near].astype(F32))
    a2a(ret_s, lambda k: ret_r.at[k], t_send, t_recv.at[0], 0, 16, -1)

    total = shared_out(x)
    s_copy(0, sh_s.at[0, top], sh_r.at[0, top], left).wait_recv()
    add_part(sh_s, (1, top), sh_r[0, top])
    go(s_copy(4, sh_s.at[1, top], sh_r.at[1, top], right))
    s_copy(1, sh_s.at[0, low_], sh_r.at[0, low_], right).wait_recv()
    add_part(sh_s, (2, low_), sh_r[0, low_])
    go(s_copy(5, sh_s.at[2, low_], sh_r.at[2, low_], left))

    own_slot = peer_of(iota((HALF, MAIN), 1) // 8) == iota((HALF, MAIN), 0)
    gather_main = one_hot(own_slot)
    gather_nine = one_hot(jnp.logical_and(own_slot, iota((HALF, MAIN), 1) % 8 == 0))
    drain(dot_r, o_recv)
    flat_dots = dot_r[...].reshape(MAIN, 128)
    p_high, p_low = halves(pick_main.astype(F32) * flat_dots[:, 0:1])
    n_high, n_low = halves(pick_nine.astype(F32) * flat_dots[:, 64:65])
    dx_s[0:HALF, :] = mm(gather_main, p_high) + mm(gather_main, p_low) + mm(gather_nine, n_high) + mm(gather_nine, n_low)
    dx_r[tp] = dx_s[...]
    for off in range(1, 8):
        remote(dx_s, dx_r.at[tp], dx_send, dx_recv, dp, (tp + off) % 8).start()

    rank_t = rank1.T.astype(BF16)
    w_high, w_low = halves(gate_w.T)
    wide_t = nt(rank_t, spread)
    gate_t = nt(w_high, spread) + nt(w_low, spread)
    weigh_main = jnp.where(wide_t == (iota((TOK, MAIN), 1) % 8 + 1).astype(F32), gate_t, 0.0)
    spread9 = one_hot(iota((HALF, 64), 1) == c * HALF + peer_of(iota((HALF, 64), 0)))
    wide9_t = nt(rank_t, spread9)
    gate9_t = nt(w_high, spread9) + nt(w_low, spread9)
    weigh_nine = jnp.where(wide9_t == float(CAP), gate9_t, 0.0)
    main_high, main_low = halves(weigh_main)
    nine_high, nine_low = halves(weigh_nine)

    drain(dx_r.at[0:7], dx_recv)
    even = dx_r[0] + dx_r[2] + dx_r[4] + dx_r[6]
    odd = dx_r[1] + dx_r[3] + dx_r[5] + dx_r[7]
    slot_dots = jnp.concatenate([even[0:HALF], odd[0:HALF]], axis=0)
    sh_dots = (even[HALF : HALF + 8] + odd[HALF : HALF + 8]).T[:, 0:1]
    taken = chosen * slot_dots
    dlogits = prob * (taken - jnp.sum(gate_w * slot_dots, axis=0, keepdims=True))
    l_high, l_low = halves(dlogits.T)
    router_q = mm(slot_expert, router[:, pl.ds(pl.multiple_of(tp * EIGHTH, 128), EIGHTH)]).astype(BF16)
    grad = mm(l_high, router_q) + mm(l_low, router_q)
    sg_cols = sgate[:, pl.ds(pl.multiple_of(tp * EIGHTH, 128), EIGHTH)]
    grad = grad + sh_dots * scale * (1.0 - scale) * sg_cols

    s_copy(2, sh_s.at[1, low_], sh_r.at[1, low_], left).wait_recv()
    s_copy(3, sh_s.at[2, top], sh_r.at[2, top], right).wait_recv()
    s_copy(4, sh_s.at[1, top], sh_r.at[1, top], left).wait_recv()
    s_copy(5, sh_s.at[2, low_], sh_r.at[2, low_], right).wait_recv()
    total = total + sh_r[1].astype(F32) + sh_r[2].astype(F32)

    drain(ret_r.at[0:16], t_recv.at[1])
    drain(ret_r.at[0:16], t_recv.at[0])
    unpack_into(xrow, ret_r[...])
    total = total + mm(main_high, xrow[0:MAIN, :]) + mm(main_low, xrow[0:MAIN, :])
    total = total + mm(nine_high, xrow[MAIN:ROWS, :]) + mm(nine_low, xrow[MAIN:ROWS, :])
    low = jnp.concatenate([total[:, 0:EIGHTH], total[:, QUARTER : QUARTER + EIGHTH]], axis=1)
    high = jnp.concatenate([total[:, EIGHTH:QUARTER], total[:, QUARTER + EIGHTH :]], axis=1)
    px_s[...] = jnp.where(c == 0, high, low)
    own = jnp.where(c == 0, low, high)
    px = remote(px_s, px_r, px_sem.at[0], px_sem.at[1], dp, x * 2 + 1 - c)
    px.start()
    px.wait_recv()
    both = own + px_r[...]
    mixed_o[...] = both[:, :EIGHTH].astype(BF16)
    grad_o[...] = (both[:, EIGHTH:] + grad).astype(BF16)

    a2a_sent(send, d_send)
    a2a_sent(ret_s, t_send)
    a2a_sent(dot_s, o_send)
    for copy in (*w_copies, *sent, px):
        copy.wait_send()
    drain(shw.at[0:7], p1_send)
    for n in range(7):
        drain(shw.at[0:4], ra_send.at[n])
        drain(shw.at[0:4], la_send.at[n if n < 6 else 7])
    drain(dx_r.at[0:7], dx_send)


def shards(
    tokens, grad_out, route_ids, expert_map, router, shared_gate, sh_gate, sh_up, sh_down, ex_gate, ex_up, ex_down
):
    vmem = pl.BlockSpec(memory_space=pltpu.VMEM)
    hbm = pl.BlockSpec(memory_space=pl.ANY)
    dma = pltpu.SemaphoreType.DMA
    block = (HALF, 8, PACK)
    return pl.pallas_call(
        body,
        out_shape=(jax.ShapeDtypeStruct((TOK, EIGHTH), BF16), jax.ShapeDtypeStruct((TOK, EIGHTH), BF16)),
        in_specs=[vmem] * 9 + [hbm] * 3,
        out_specs=(vmem, vmem),
        scratch_shapes=[
            pltpu.VMEM(block, BF16),
            pltpu.VMEM((XS, *block), BF16),
            pltpu.VMEM((2, HID, WIDTH), BF16),
            pltpu.VMEM((2, HID, WIDTH), BF16),
            pltpu.VMEM((2, HID, WIDTH), BF16),
            pltpu.VMEM((ROWS, 2 * QUARTER), BF16),
            pltpu.VMEM((6, ROWS, HID), F32),
            pltpu.VMEM((2, ROWS, HID), BF16),
            pltpu.VMEM((2, ROWS, HID), BF16),
            pltpu.VMEM((2, ROWS, HID), BF16),
            pltpu.VMEM((3, *block), BF16),
            pltpu.VMEM((2, 8, 8, PACK), BF16),
            pltpu.VMEM((2, 8, 8, PACK), BF16),
            pltpu.VMEM(block, BF16),
            pltpu.VMEM(block, BF16),
            pltpu.VMEM(block, BF16),
            pltpu.VMEM(block, BF16),
            pltpu.VMEM((RING * RING, 32, 3 * SPAD), BF16),
            pltpu.VMEM((32, 3 * SPAD), BF16),
            pltpu.VMEM((1, WIDTH), F32),
            pltpu.VMEM((3, TOK, 2 * QUARTER), BF16),
            pltpu.VMEM((3, TOK, 2 * QUARTER), BF16),
            pltpu.VMEM((TOK, QUARTER), F32),
            pltpu.VMEM((TOK, QUARTER), F32),
            pltpu.VMEM((HALF + 8, TOK), F32),
            pltpu.VMEM((8, HALF + 8, TOK), F32),
            pltpu.VMEM((3, TOK, SHID), F32),
            pltpu.VMEM((HALF, 8, 128), F32),
            pltpu.VMEM((HALF, 8, 128), F32),
            dma((4,)), dma((3,)), dma((3,)), dma, dma((2,)), dma((12,)), dma((12,)), dma((12,)), dma((12,)),
            dma, dma((2,)), dma, dma, dma((8,)), dma((8,)), dma((8,)), dma((8,)),
            dma((6,)), dma((6,)), dma((2,)), dma, dma, dma, dma,
        ],
        compiler_params=pltpu.CompilerParams(
            collective_id=0, has_side_effects=True, vmem_limit_bytes=60 * 1024 * 1024
        ),
    )(
        tokens, grad_out, route_ids.T, expert_map.reshape(1, 60), router.T, shared_gate.reshape(16, 128),
        sh_gate, sh_up, sh_down.T,
        ex_gate.reshape(WIDTH, HID).T, ex_up.reshape(WIDTH, HID).T, ex_down.reshape(HID, WIDTH),
    )


def solution(mesh):
    placed = (
        P("dp", None), P("dp", None), P("dp", None), P(), P(), P(),
        P("dp", "tensor"), P("dp", "tensor"), P("tensor", "dp"),
        P("dp", None, "tensor"), P("dp", None, "tensor"), P("dp", "tensor", None),
    )
    return jax.shard_map(
        shards,
        mesh=mesh,
        in_specs=placed,
        out_specs=(P("dp", "tensor"), P("dp", "tensor")),
        check_vma=False,
    )
```

time: 128 us -> 104 us (0.81)
  Pallas kernels: 115 us -> 101 us
  local copies, waits for them, and re-layouts: 11.2 us -> 2.14 us
  other arithmetic: 1.4 us -> 0 us
    pallas_call x1, Pallas kernels: 115 us -> 101 us  [shards(): pl.pallas_call(body, out_shape=(jax.ShapeDtypeStruct((TOK, EIGHTH), BF16)...]
    unnamed x10 -> x4, local copies, waits for them, and re-layouts: 5.69 us -> 2.14 us
    pad x2 -> x0, local copies, waits for them, and re-layouts: 2.97 us -> none  [the longest x1 1.69 us: shards(): router_t = jnp.pad(router.T, ((0, 4), (0, 0)))]
    reshape x2 -> x0, local copies, waits for them, and re-layouts: 2.53 us -> none  [the longest x1 1.29 us: shards(): shared_gate.reshape(1, WIDTH)]
    concatenate x1 -> x0, other arithmetic: 1.4 us -> none  [shards(): jnp.concatenate([jnp.pad(a, ((0, 0), (0, SPAD - SHID))) for a in (sh_gate...]
where the time goes in v2:
time: 104 us
  Pallas kernels  101 us (97%)
  local copies, waits for them, and re-layouts  2.14 us (2%)
    pallas_call x1, Pallas kernels, shards(): pl.pallas_call(body, out_shape=(jax.ShapeDtypeStruct((TOK, EIGHTH), BF16)...  101 us
    unnamed x4, local copies, waits for them, and re-layouts  2.14 us

profile of v2, /device:TPU:1, one launch (start us, length us, event | category | flops | bytes accessed | tf_op | source)
XLA Modules:
  0.0 103.6 jit_solution(14677528448344528210)
XLA Ops:
  0.6 100.8 %shard_map.131 = (bf16[128,256]{1,0:T(8,128)(2,1)}, bf16[128,256]{1,0:T(8,128)(2,1)}) custom-call(bf16[128,2048]{1,0:T(8,128)(2,1)} %tok.1, bf16[128,2048]{1,0:T(8,128)(2,1)} %cot.1, s32[4,128]{1,0:T(4,128)} %bitcast.18, s32[1,60]{1,0:T(1,128)} %bitcast.19, bf16[60,2048]{1,0:T(8,128)(2,1)} %bitcast.15, bf16[16,128]{1,0:T(8,128)(2,1)} %bitcast.17, ...), custom_call_target="tpu_custom_call" | custom-call | tf_op jit(solution)/shard_map/pallas_call | solution.py:521
  101.4 0.0 copy-start
  101.4 1.5 %copy.16 = bf16[128,256]{1,0:T(8,128)(2,1)} copy(bf16[128,256]{1,0:T(8,128)(2,1)} %get-tuple-element.4) | data formatting | bytes 131072
  102.9 0.0 copy-done
  103.0 0.6 copy.17
Async XLA Ops:
  101.4 1.5 %copy-start = (bf16[128,256]{1,0:T(8,128)(2,1)S(1)}, bf16[128,256]{1,0:T(8,128)(2,1)}, u32[]{:S(2)}) copy-start(bf16[128,256]{1,0:T(8,128)(2,1)} %get-tuple-element.5) | copy-start | bytes 196612

commit v3 on v2

--- a/solution.py
+++ b/solution.py
@@ -21,6 +21,8 @@
 SHID = 352
 SPAD = 384
 MAIN = HALF * 8
+OWN = 16
+SETS = 4
 ROWS = HALF * CAP
 
 
@@ -70,12 +72,12 @@
 
 def body(
     tok, cot, ids, emap, router, sgate_in, sh_gate, sh_up, sh_down, wg_in, wu_in, wd_in,
-    mixed_o, grad_o,
+    result,
     send, gat, wg, wu, wd, xrow, acc, hid, gg, gu, outs, rs_a, rs_b, rs_l, rs_r,
-    ret_s, ret_r, shw, sh_own, sgate, sh_s, sh_r, px_s, px_r, dx_s, dx_r, sh_acc, dot_s, dot_r,
+    ret_s, ret_r, shw, sh_own, sgate, sh_s, sh_r, px_s, px_r, dx_s, dx_r, sh_acc, dot_s, dot_r, sx_s, sx_r,
     local_sem, w_send, w_recv, d_send, d_recv, x_send, x_recv, rs_send, rs_recv,
-    t_send, t_recv, p1_send, p1_recv, ra_send, ra_recv, la_send, la_recv,
-    s_send, s_recv, px_sem, dx_send, dx_recv, o_send, o_recv,
+    t_send, t_recv, pr_send, pr_recv, pl_send, pl_recv, ra_send, ra_recv, la_send, la_recv,
+    s_send, s_recv, px_sem, dx_send, dx_recv, o_send, o_recv, sx_send, sx_recv,
 ):
     dp = lax.axis_index("dp")
     tp = lax.axis_index("tensor")
@@ -95,11 +97,10 @@
     def line(a, b):
         return a * (1 + 7 * c) + b * (8 - 7 * c)
 
-    def offset(k):
-        return jnp.where(k % 2 == 0, k // 2, HALF - (k + 1) // 2)
-
-    def peer_of(k):
-        return (mine + offset(k)) % HALF
+    def peer_of(k, sign=1):
+        j = k // 4
+        dz = jnp.where(j < 2, 1 + 4 * j, jnp.where(j < 4, 15 - 4 * j, jnp.where(j < 6, 4 * j - 16, 4 * j - 22)))
+        return ((zc + sign * dz + RING) % RING) * 4 + (yc // 2 + sign * (k % 4) + 4) % 4
 
     def remote(src, dst, ssem, rsem, d, t):
         return pltpu.make_async_remote_copy(
@@ -126,11 +127,12 @@
     lax.fori_loop(0, HALF, greet_peer, 0)
     for off in range(1, 8):
         greet(dp, (tp + off) % 8)
-        greet(line((a_me + off) % RING, b_me), tp)
     b_right = line(a_me, (b_me + 1) % RING)
     b_left = line(a_me, (b_me + 7) % RING)
-    greet(b_right, tp)
-    greet(b_left, tp)
+    a_right = line((a_me + 1) % RING, b_me)
+    a_left = line((a_me + 7) % RING, b_me)
+    for d in (a_right, a_left, b_right, b_left):
+        greet(d, tp)
 
     loads = [
         pltpu.make_async_copy(wg_in, wg.at[0], local_sem.at[0]),
@@ -168,12 +170,12 @@
     send[:, :, : 2 * QUARTER] = block.astype(BF16)
     send[:, :, 2 * QUARTER :] = extra.astype(BF16)
 
-    pl.semaphore_wait(barrier, HALF + 16 - to_self.astype(jnp.int32))
+    pl.semaphore_wait(barrier, HALF + 11 - to_self.astype(jnp.int32))
 
     def a2a(src, dst, ssem, rsem, lo, hi, sign):
         def step(k, carry):
-            i = (mine + sign * offset(k) + HALF) % HALF
-            own = jnp.logical_and(k == 0, to_self)
+            i = peer_of(k, sign)
+            own = jnp.logical_and(k == OWN, to_self)
 
             @pl.when(own)
             def _():
@@ -196,10 +198,28 @@
         def _():
             drain(src, ssem)
 
-    a2a(send, lambda k: gat.at[x, k], d_send, d_recv.at[0], 0, 16, 1)
-    a2a(send, lambda k: gat.at[x, k], d_send, d_recv.at[1], 16, HALF, 1)
+    def line_step(k):
+        lo, hi = (slice(0, 32), slice(0, 32)) if k < 4 else (slice(0, 16), slice(16, 32))
+        at_r = line((a_me + RING - (k - 1)) % RING, b_me)
+        at_l = line((a_me + k - 1) % RING, b_me)
+        src_r, src_l = (sh_own, sh_own) if k == 1 else (shw.at[at_r], shw.at[at_l])
+        remote(src_r.at[lo], shw.at[at_r, lo], pr_send.at[k - 1], pr_recv.at[k - 1], a_right, tp).start()
+        remote(src_l.at[hi], shw.at[at_l, hi], pl_send.at[k - 1], pl_recv.at[k - 1], a_left, tp).start()
+
+    def line_wait(k):
+        part = shw.at[0] if k < 4 else shw.at[0, 0:16]
+        drain(part, pr_recv.at[k - 1])
+        drain(part, pl_recv.at[k - 1])
+
+    def dispatch(g):
+        a2a(send, lambda k: gat.at[x, k], d_send, d_recv.at[g], 8 * g, 8 * g + 8, 1)
 
     loads[3].start()
+    line_step(1)
+    dispatch(0)
+    line_wait(1)
+    line_step(2)
+    dispatch(1)
 
     w_copies = [
         remote(wg_in, wg.at[1], w_send.at[0], w_recv.at[0], dp, x * 2 + 1 - c),
@@ -208,8 +228,6 @@
     ]
     for copy in w_copies:
         copy.start()
-    for off in range(1, 8):
-        remote(sh_own, shw.at[dp], p1_send, p1_recv, line((a_me + off) % RING, b_me), tp).start()
 
     router_s = mm(slot_expert, router[...]).astype(BF16)
     logits = nt(router_s, tok[...])
@@ -221,58 +239,31 @@
         1.0 + jnp.exp(-jnp.sum(tok[...].astype(F32) * sgate[...], axis=1, keepdims=True))
     )
 
-    h = [slice(8 * n, 8 * n + 8) for n in range(4)]
-
-    def x_copy(n, q, part, t):
-        return remote(gat.at[q, part], gat.at[q, part], x_send.at[n], x_recv.at[n], dp, t)
-
     sent = []
 
     def go(copy):
         copy.start()
         sent.append(copy)
 
-    def x_first(n, part, other):
-        drain(gat.at[x, 0:16], d_recv.at[n // 6])
-        go(x_copy(n, x, part, right))
-        go(x_copy(n + 1, x, other, left))
-        go(x_copy(n + 2, x, other, right))
-        go(x_copy(n + 3, x, part, left))
-
-    def x_forward(n, part, other):
-        x_copy(n, x3, part, left).wait_recv()
-        go(x_copy(n + 4, x3, part, right))
-        x_copy(n + 1, x1, other, right).wait_recv()
-        go(x_copy(n + 5, x1, other, left))
-
-    x_first(0, h[0], h[1])
-    x_forward(0, h[0], h[1])
-    x_first(6, h[2], h[3])
-
-    loads[3].wait()
-    drain(shw.at[0:7], p1_recv)
-
-    def line_send(b, half, ssem, rsem, target):
-        for a in range(4 * half, 4 * half + 4):
-            at_ = line(a, b % RING)
-            remote(shw.at[at_], shw.at[at_], ssem, rsem, target, tp).start()
-
-    def ring_step(k, half):
-        n = 2 * (k - 1) + half
-        if k > 1:
-            drain(shw.at[0:4], ra_recv.at[n - 2])
-            drain(shw.at[0:4], la_recv.at[n - 2])
-        if k < 4 or half == 0:
-            line_send(b_me + RING - (k - 1), half, ra_send.at[n], ra_recv.at[n], b_right)
-        if k < 4 or half == 1:
-            line_send(b_me + (k - 1), half, la_send.at[n], la_recv.at[n], b_left)
-
-    ring_step(1, 0)
-    ring_step(1, 1)
-    for copy in loads[:3]:
-        copy.wait()
-    for copy in w_copies:
-        copy.wait_recv()
+    def part(g, n):
+        return slice(8 * g + 4 * n, 8 * g + 4 * n + 4)
+
+    def x_copy(g, n, q, half, t):
+        at = part(g, half)
+        return remote(gat.at[q, at], gat.at[q, at], x_send.at[6 * g + n], x_recv.at[6 * g + n], dp, t)
+
+    def x_first(g):
+        drain(gat.at[x, 0:8], d_recv.at[g])
+        go(x_copy(g, 0, x, 0, right))
+        go(x_copy(g, 1, x, 1, left))
+        go(x_copy(g, 2, x, 1, right))
+        go(x_copy(g, 3, x, 0, left))
+
+    def x_forward(g):
+        x_copy(g, 0, x3, 0, left).wait_recv()
+        go(x_copy(g, 4, x3, 0, right))
+        x_copy(g, 1, x1, 1, right).wait_recv()
+        go(x_copy(g, 5, x1, 1, left))
 
     def feed(q, start):
         unpack_into(xrow, gat[q])
@@ -289,20 +280,57 @@
                 else:
                     acc[3 * p + n] += part
 
-    x_copy(2, x3, h[1], left).wait_recv()
-    x_copy(3, x1, h[0], right).wait_recv()
-    x_copy(4, x2, h[0], left).wait_recv()
-    x_copy(5, x2, h[1], right).wait_recv()
+    def line_send(b, half, ssem, rsem, target):
+        for off in ((2, 5, 3, 4) if half else (0, 7, 1, 6)):
+            at_ = line((a_me + off) % RING, b % RING)
+            remote(shw.at[at_], shw.at[at_], ssem, rsem, target, tp).start()
+
+    def ring_step(k, half):
+        n = 2 * (k - 1) + half
+        if k > 1:
+            drain(shw.at[0:4], ra_recv.at[n - 2])
+            drain(shw.at[0:4], la_recv.at[n - 2])
+        if k < 4 or half == 0:
+            line_send(b_me + RING - (k - 1), half, ra_send.at[n], ra_recv.at[n], b_right)
+        if k < 4 or half == 1:
+            line_send(b_me + (k - 1), half, la_send.at[n], la_recv.at[n], b_left)
+
+    line_wait(2)
+    line_step(3)
+    dispatch(2)
+    x_first(0)
+    line_wait(3)
+    line_step(4)
+    dispatch(3)
+    loads[3].wait()
+    ring_step(1, 0)
+    x_forward(0)
+    x_first(1)
+    line_wait(4)
+    ring_step(1, 1)
+    x_forward(1)
+    x_first(2)
+    ring_step(2, 0)
+    x_forward(2)
+    for copy in loads[:3]:
+        copy.wait()
+    for copy in w_copies:
+        copy.wait_recv()
+    x_first(3)
+    ring_step(2, 1)
     feed(x, True)
-    x_forward(6, h[2], h[3])
-    ring_step(2, 0)
-    ring_step(2, 1)
-    x_copy(8, x3, h[3], left).wait_recv()
+    x_forward(3)
+    ring_step(3, 0)
+    for g in range(SETS):
+        x_copy(g, 2, x3, 1, left).wait_recv()
     feed(x3, False)
-    x_copy(9, x1, h[2], right).wait_recv()
+    for g in range(SETS):
+        x_copy(g, 3, x1, 0, right).wait_recv()
     feed(x1, False)
-    x_copy(10, x2, h[2], left).wait_recv()
-    x_copy(11, x2, h[3], right).wait_recv()
+    ring_step(3, 1)
+    for g in range(SETS):
+        x_copy(g, 4, x2, 0, left).wait_recv()
+        x_copy(g, 5, x2, 1, right).wait_recv()
     feed(x2, False)
 
     row_dots = jnp.zeros((ROWS, 1), F32)
@@ -328,52 +356,90 @@
         ref[:, :, : 2 * QUARTER] = packed[0].astype(BF16)
         ref[:, :, 2 * QUARTER :] = packed[1].astype(BF16)
 
-    def rs_copy(n, src, dst, t):
-        return remote(src, dst, rs_send.at[n], rs_recv.at[n], dp, t)
-
     def add_part(ref, at, more):
         ref[at] = (ref[at].astype(F32) + more.astype(F32)).astype(BF16)
 
+    def rs_copy(g, n):
+        at = part(g, n % 2)
+        src, dst, t = (
+            (outs.at[0, at], rs_a.at[g], right),
+            (outs.at[0, at], rs_b.at[g], left),
+            (outs.at[1, part(g, 1)], rs_l.at[part(g, 1)], right),
+            (outs.at[2, part(g, 0)], rs_r.at[part(g, 0)], left),
+            (outs.at[1, at], rs_l.at[at], right),
+            (outs.at[2, at], rs_r.at[at], left),
+        )[n]
+        return remote(src, dst, rs_send.at[6 * g + n], rs_recv.at[6 * g + n], dp, t)
+
+    def rs_start(g):
+        go(rs_copy(g, 0))
+        go(rs_copy(g, 1))
+
+    def rs_free(g):
+        go(rs_copy(g, 2))
+        go(rs_copy(g, 3))
+
+    def rs_forward(g):
+        rs_copy(g, 0).wait_recv()
+        add_part(outs, (1, part(g, 0)), rs_a[g])
+        go(rs_copy(g, 4))
+        rs_copy(g, 1).wait_recv()
+        add_part(outs, (2, part(g, 1)), rs_b[g])
+        go(rs_copy(g, 5))
+
+    def give_back(g):
+        for n in range(2, 6):
+            rs_copy(g, n).wait_recv()
+        at = slice(8 * g, 8 * g + 8)
+        add_part(ret_s, at, rs_l[at].astype(F32) + rs_r[at].astype(F32))
+        a2a(ret_s, lambda k: ret_r.at[k], t_send, t_recv.at[g], 8 * g, 8 * g + 8, -1)
+
     put(outs.at[0], produce(x2))
-    go(rs_copy(0, outs.at[0, h[2]], rs_a.at[0], right))
-    go(rs_copy(1, outs.at[0, h[3]], rs_b.at[0], left))
+    rs_start(0)
+    ring_step(4, 0)
     put(outs.at[1], produce(x1))
-    go(rs_copy(2, outs.at[1, h[3]], rs_l.at[h[3]], right))
+    go(rs_copy(0, 2))
     put(outs.at[2], produce(x3))
-    go(rs_copy(3, outs.at[2, h[2]], rs_r.at[h[2]], left))
+    go(rs_copy(0, 3))
+    rs_start(1)
+    ring_step(4, 1)
 
     n_high, n_low = halves(jnp.broadcast_to(row_dots[MAIN:], (HALF, 128)))
-    ninth_dots = mm(repeat, n_high) + mm(repeat, n_low)
-    both_dots = jnp.where(iota((MAIN, 128), 1) < 64, jnp.broadcast_to(row_dots[:MAIN], (MAIN, 128)), ninth_dots)
-    dot_s[...] = both_dots.reshape(HALF, 8, 128)
-
+    m_high, m_low = halves(jnp.broadcast_to(row_dots[:MAIN], (MAIN, 128)))
+    lane = iota((MAIN, 128), 1) // 32
+    both_dots = jnp.where(lane == 2, mm(repeat, n_high), mm(repeat, n_low))
+    both_dots = jnp.where(lane == 0, m_high.astype(F32), jnp.where(lane == 1, m_low.astype(F32), both_dots))
+    dot_s[...] = both_dots.reshape(HALF, 8, 128).astype(BF16)
     put(ret_s, produce(x))
     a2a(dot_s, lambda k: dot_r.at[k], o_send, o_recv, 0, HALF, -1)
-    ring_step(3, 0)
-    rs_copy(0, outs.at[0, h[2]], rs_a.at[0], left).wait_recv()
-    add_part(outs, (1, h[2]), rs_a[0])
-    go(rs_copy(4, outs.at[1, h[2]], rs_l.at[h[2]], right))
-    rs_copy(1, outs.at[0, h[3]], rs_b.at[0], right).wait_recv()
-    add_part(outs, (2, h[3]), rs_b[0])
-    go(rs_copy(5, outs.at[2, h[3]], rs_r.at[h[3]], left))
-    go(rs_copy(6, outs.at[0, h[0]], rs_a.at[1], right))
-    go(rs_copy(7, outs.at[0, h[1]], rs_b.at[1], left))
-    go(rs_copy(8, outs.at[1, h[1]], rs_l.at[h[1]], right))
-    go(rs_copy(9, outs.at[2, h[0]], rs_r.at[h[0]], left))
-    ring_step(3, 1)
-    ring_step(4, 0)
-
-    far, near = slice(16, HALF), slice(0, 16)
-    for n, part in ((2, h[3]), (4, h[2])):
-        rs_copy(n, outs.at[1, part], rs_l.at[part], left).wait_recv()
-    for n, part in ((3, h[2]), (5, h[3])):
-        rs_copy(n, outs.at[2, part], rs_r.at[part], right).wait_recv()
-    add_part(ret_s, far, rs_l[far].astype(F32) + rs_r[far].astype(F32))
-    a2a(ret_s, lambda k: ret_r.at[k], t_send, t_recv.at[1], 16, HALF, -1)
-    ring_step(4, 1)
+
+    rs_forward(0)
+    rs_free(1)
+    rs_start(2)
+    rs_forward(1)
+    rs_free(2)
+    rs_start(3)
+    rs_forward(2)
+    rs_free(3)
 
     drain(shw.at[0:4], ra_recv.at[6])
     drain(shw.at[0:4], la_recv.at[7])
+    give_back(0)
+    give_back(1)
+
+    own_slot = peer_of(iota((HALF, MAIN), 1) // 8) == iota((HALF, MAIN), 0)
+    gather_main = one_hot(own_slot)
+    gather_nine = one_hot(jnp.logical_and(own_slot, iota((HALF, MAIN), 1) % 8 == 0))
+    drain(dot_r, o_recv)
+    flat_dots = dot_r[...].astype(F32).reshape(MAIN, 128)
+    p_high, p_low = halves(pick_main.astype(F32) * (flat_dots[:, 0:1] + flat_dots[:, 32:33]))
+    n_high, n_low = halves(pick_nine.astype(F32) * (flat_dots[:, 64:65] + flat_dots[:, 96:97]))
+    dx_s[...] = (
+        mm(gather_main, p_high) + mm(gather_main, p_low) + mm(gather_nine, n_high) + mm(gather_nine, n_low)
+    )
+    dx_r[tp] = dx_s[...]
+    for off in range(1, 8):
+        remote(dx_s, dx_r.at[tp], dx_send, dx_recv, dp, (tp + off) % 8).start()
 
     def shared_in(n, carry):
         cols = pl.ds(pl.multiple_of(n * QUARTER, 128), QUARTER)
@@ -387,13 +453,6 @@
             sh_acc[m] = part + jnp.where(n == 0, 0.0, 1.0) * sh_acc[m]
         return carry
 
-    rs_copy(6, outs.at[0, h[0]], rs_a.at[1], left).wait_recv()
-    add_part(outs, (1, h[0]), rs_a[1])
-    go(rs_copy(10, outs.at[1, h[0]], rs_l.at[h[0]], right))
-    rs_copy(7, outs.at[0, h[1]], rs_b.at[1], right).wait_recv()
-    add_part(outs, (2, h[1]), rs_b[1])
-    go(rs_copy(11, outs.at[2, h[1]], rs_r.at[h[1]], left))
-
     for m in range(3):
         sh_acc[m] = jnp.zeros((TOK, SHID), F32)
     lax.fori_loop(0, XS, shared_in, 0)
@@ -404,7 +463,13 @@
     sh_gu = (sh_grad * active).astype(BF16)
     dot_high, dot_low = halves(sh_hid.astype(F32) * sh_grad)
     ones_s = jnp.ones((8, SHID), BF16)
-    dx_s[HALF : HALF + 8, :] = nt(ones_s, dot_high) + nt(ones_s, dot_low)
+    sx_s[...] = nt(ones_s, dot_high) + nt(ones_s, dot_low)
+    sx_r[tp] = sx_s[...]
+    for off in range(1, 8):
+        remote(sx_s, sx_r.at[tp], sx_send, sx_recv, dp, (tp + off) % 8).start()
+
+    rs_forward(3)
+    give_back(2)
 
     def shared_out(q):
         blocks = pl.ds(q * 16, 16)
@@ -425,32 +490,15 @@
     sh_s[2] = shared_out(x3).astype(BF16)
     go(s_copy(3, sh_s.at[2, top], sh_r.at[2, top], left))
 
-    for n, part in ((8, h[1]), (10, h[0])):
-        rs_copy(n, outs.at[1, part], rs_l.at[part], left).wait_recv()
-    for n, part in ((9, h[0]), (11, h[1])):
-        rs_copy(n, outs.at[2, part], rs_r.at[part], right).wait_recv()
-    add_part(ret_s, near, rs_l[near].astype(F32) + rs_r[near].astype(F32))
-    a2a(ret_s, lambda k: ret_r.at[k], t_send, t_recv.at[0], 0, 16, -1)
-
+    give_back(3)
     total = shared_out(x)
+
     s_copy(0, sh_s.at[0, top], sh_r.at[0, top], left).wait_recv()
     add_part(sh_s, (1, top), sh_r[0, top])
     go(s_copy(4, sh_s.at[1, top], sh_r.at[1, top], right))
     s_copy(1, sh_s.at[0, low_], sh_r.at[0, low_], right).wait_recv()
     add_part(sh_s, (2, low_), sh_r[0, low_])
     go(s_copy(5, sh_s.at[2, low_], sh_r.at[2, low_], left))
-
-    own_slot = peer_of(iota((HALF, MAIN), 1) // 8) == iota((HALF, MAIN), 0)
-    gather_main = one_hot(own_slot)
-    gather_nine = one_hot(jnp.logical_and(own_slot, iota((HALF, MAIN), 1) % 8 == 0))
-    drain(dot_r, o_recv)
-    flat_dots = dot_r[...].reshape(MAIN, 128)
-    p_high, p_low = halves(pick_main.astype(F32) * flat_dots[:, 0:1])
-    n_high, n_low = halves(pick_nine.astype(F32) * flat_dots[:, 64:65])
-    dx_s[0:HALF, :] = mm(gather_main, p_high) + mm(gather_main, p_low) + mm(gather_nine, n_high) + mm(gather_nine, n_low)
-    dx_r[tp] = dx_s[...]
-    for off in range(1, 8):
-        remote(dx_s, dx_r.at[tp], dx_send, dx_recv, dp, (tp + off) % 8).start()
 
     rank_t = rank1.T.astype(BF16)
     w_high, w_low = halves(gate_w.T)
@@ -467,8 +515,9 @@
     drain(dx_r.at[0:7], dx_recv)
     even = dx_r[0] + dx_r[2] + dx_r[4] + dx_r[6]
     odd = dx_r[1] + dx_r[3] + dx_r[5] + dx_r[7]
-    slot_dots = jnp.concatenate([even[0:HALF], odd[0:HALF]], axis=0)
-    sh_dots = (even[HALF : HALF + 8] + odd[HALF : HALF + 8]).T[:, 0:1]
+    slot_dots = jnp.concatenate([even, odd], axis=0)
+    drain(sx_r.at[0:7], sx_recv)
+    sh_dots = jnp.sum(sx_r[...], axis=0).T[:, 0:1]
     taken = chosen * slot_dots
     dlogits = prob * (taken - jnp.sum(gate_w * slot_dots, axis=0, keepdims=True))
     l_high, l_low = halves(dlogits.T)
@@ -483,8 +532,8 @@
     s_copy(5, sh_s.at[2, low_], sh_r.at[2, low_], right).wait_recv()
     total = total + sh_r[1].astype(F32) + sh_r[2].astype(F32)
 
-    drain(ret_r.at[0:16], t_recv.at[1])
-    drain(ret_r.at[0:16], t_recv.at[0])
+    for g in range(SETS):
+        drain(ret_r.at[0:8], t_recv.at[g])
     unpack_into(xrow, ret_r[...])
     total = total + mm(main_high, xrow[0:MAIN, :]) + mm(main_low, xrow[0:MAIN, :])
     total = total + mm(nine_high, xrow[MAIN:ROWS, :]) + mm(nine_low, xrow[MAIN:ROWS, :])
@@ -496,19 +545,23 @@
     px.start()
     px.wait_recv()
     both = own + px_r[...]
-    mixed_o[...] = both[:, :EIGHTH].astype(BF16)
-    grad_o[...] = (both[:, EIGHTH:] + grad).astype(BF16)
+    result[:, :EIGHTH] = both[:, :EIGHTH]
+    result[:, EIGHTH:] = both[:, EIGHTH:] + grad
 
     a2a_sent(send, d_send)
     a2a_sent(ret_s, t_send)
     a2a_sent(dot_s, o_send)
     for copy in (*w_copies, *sent, px):
         copy.wait_send()
-    drain(shw.at[0:7], p1_send)
+    for k in range(4):
+        part = shw.at[0] if k < 3 else shw.at[0, 0:16]
+        drain(part, pr_send.at[k])
+        drain(part, pl_send.at[k])
     for n in range(7):
         drain(shw.at[0:4], ra_send.at[n])
         drain(shw.at[0:4], la_send.at[n if n < 6 else 7])
     drain(dx_r.at[0:7], dx_send)
+    drain(sx_r.at[0:7], sx_send)
 
 
 def shards(
@@ -518,11 +571,11 @@
     hbm = pl.BlockSpec(memory_space=pl.ANY)
     dma = pltpu.SemaphoreType.DMA
     block = (HALF, 8, PACK)
-    return pl.pallas_call(
+    sums = pl.pallas_call(
         body,
-        out_shape=(jax.ShapeDtypeStruct((TOK, EIGHTH), BF16), jax.ShapeDtypeStruct((TOK, EIGHTH), BF16)),
+        out_shape=jax.ShapeDtypeStruct((TOK, QUARTER), F32),
         in_specs=[vmem] * 9 + [hbm] * 3,
-        out_specs=(vmem, vmem),
+        out_specs=vmem,
         scratch_shapes=[
             pltpu.VMEM(block, BF16),
             pltpu.VMEM((XS, *block), BF16),
@@ -535,8 +588,8 @@
             pltpu.VMEM((2, ROWS, HID), BF16),
             pltpu.VMEM((2, ROWS, HID), BF16),
             pltpu.VMEM((3, *block), BF16),
-            pltpu.VMEM((2, 8, 8, PACK), BF16),
-            pltpu.VMEM((2, 8, 8, PACK), BF16),
+            pltpu.VMEM((SETS, 4, 8, PACK), BF16),
+            pltpu.VMEM((SETS, 4, 8, PACK), BF16),
             pltpu.VMEM(block, BF16),
             pltpu.VMEM(block, BF16),
             pltpu.VMEM(block, BF16),
@@ -548,14 +601,16 @@
             pltpu.VMEM((3, TOK, 2 * QUARTER), BF16),
             pltpu.VMEM((TOK, QUARTER), F32),
             pltpu.VMEM((TOK, QUARTER), F32),
-            pltpu.VMEM((HALF + 8, TOK), F32),
-            pltpu.VMEM((8, HALF + 8, TOK), F32),
+            pltpu.VMEM((HALF, TOK), F32),
+            pltpu.VMEM((8, HALF, TOK), F32),
             pltpu.VMEM((3, TOK, SHID), F32),
-            pltpu.VMEM((HALF, 8, 128), F32),
-            pltpu.VMEM((HALF, 8, 128), F32),
-            dma((4,)), dma((3,)), dma((3,)), dma, dma((2,)), dma((12,)), dma((12,)), dma((12,)), dma((12,)),
-            dma, dma((2,)), dma, dma, dma((8,)), dma((8,)), dma((8,)), dma((8,)),
-            dma((6,)), dma((6,)), dma((2,)), dma, dma, dma, dma,
+            pltpu.VMEM((HALF, 8, 128), BF16),
+            pltpu.VMEM((HALF, 8, 128), BF16),
+            pltpu.VMEM((8, TOK), F32),
+            pltpu.VMEM((8, 8, TOK), F32),
+            dma((4,)), dma((3,)), dma((3,)), dma, dma((4,)), dma((24,)), dma((24,)), dma((24,)), dma((24,)),
+            dma, dma((4,)), dma((4,)), dma((4,)), dma((4,)), dma((4,)), dma((8,)), dma((8,)), dma((8,)), dma((8,)),
+            dma((6,)), dma((6,)), dma((2,)), dma, dma, dma, dma, dma, dma,
         ],
         compiler_params=pltpu.CompilerParams(
             collective_id=0, has_side_effects=True, vmem_limit_bytes=60 * 1024 * 1024
@@ -565,6 +620,7 @@
         sh_gate, sh_up, sh_down.T,
         ex_gate.reshape(WIDTH, HID).T, ex_up.reshape(WIDTH, HID).T, ex_down.reshape(HID, WIDTH),
     )
+    return sums[:, :EIGHTH].astype(BF16), sums[:, EIGHTH:].astype(BF16)
 
 
 def solution(mesh):

time: 104 us -> 94.9 us (0.913)
  Pallas kernels: 101 us -> 92.5 us
  local copies, waits for them, and re-layouts: 2.14 us -> 0.66 us
    pallas_call x1, Pallas kernels: 101 us -> 92.5 us  [shards(): pl.pallas_call(body, out_shape=jax.ShapeDtypeStruct((TOK, QUARTER), F32),...]
    unnamed x4 -> x0, local copies, waits for them, and re-layouts: 2.14 us -> none
where the time goes in v3:
time: 94.9 us; the launch traced here: 94.7 us
  Pallas kernels  92.5 us (97%)
  other arithmetic  0.97 us (1%)
    pallas_call x1, Pallas kernels, shards(): pl.pallas_call(body, out_shape=jax.ShapeDtypeStruct((TOK, QUARTER), F32),...  92.5 us

profile of v3, /device:TPU:1, one launch (start us, length us, event | category | flops | bytes accessed | tf_op | source)
XLA Modules:
  0.0 94.7 jit_solution(5338460000919905176)
XLA Ops:
  0.6 92.5 %shard_map.131 = f32[128,512]{1,0:T(8,128)} custom-call(bf16[128,2048]{1,0:T(8,128)(2,1)} %tok.1, bf16[128,2048]{1,0:T(8,128)(2,1)} %cot.1, s32[4,128]{1,0:T(4,128)} %bitcast.18, s32[1,60]{1,0:T(1,128)} %bitcast.19, bf16[60,2048]{1,0:T(8,128)(2,1)} %bitcast.15, bf16[16,128]{1,0:T(8,128)(2,1)} %bitcast.17, bf16[32,352]{1,0:T(8,128)(2,1)} %sh_gate.1, ...), custom_call_target="tpu_custom_call" | custom-call | tf_op jit(solution)/shard_map/pallas_call | solution.py:574
  93.1 1.0 %convert.4 = bf16[128,512]{1,0:T(8,128)(2,1)S(1)} convert(f32[128,512]{1,0:T(8,128)} %shard_map.131) | non-fusion elementwise | flops 65536 | bytes 393216 | tf_op jit(solution)/shard_map/convert.1
  94.1 0.7 fusion

commit v4 on v3

--- a/solution.py
+++ b/solution.py
@@ -74,10 +74,10 @@
     tok, cot, ids, emap, router, sgate_in, sh_gate, sh_up, sh_down, wg_in, wu_in, wd_in,
     result,
     send, gat, wg, wu, wd, xrow, acc, hid, gg, gu, outs, rs_a, rs_b, rs_l, rs_r,
-    ret_s, ret_r, shw, sh_own, sgate, sh_s, sh_r, px_s, px_r, dx_s, dx_r, sh_acc, dot_s, dot_r, sx_s, sx_r,
+    ret_s, ret_r, shw, sh_own, sgate, sh_s, sh_r, keep, ps_s, ps_r, px_s, px_r, dx_s, dx_r, sh_acc, dot_s, dot_r, sx_s, sx_r,
     local_sem, w_send, w_recv, d_send, d_recv, x_send, x_recv, rs_send, rs_recv,
     t_send, t_recv, pr_send, pr_recv, pl_send, pl_recv, ra_send, ra_recv, la_send, la_recv,
-    s_send, s_recv, px_sem, dx_send, dx_recv, o_send, o_recv, sx_send, sx_recv,
+    s_send, s_recv, px_sem, dx_send, dx_recv, o_send, o_recv, sx_send, sx_recv, ps_send, ps_recv,
 ):
     dp = lax.axis_index("dp")
     tp = lax.axis_index("tensor")
@@ -308,15 +308,15 @@
     x_first(1)
     line_wait(4)
     ring_step(1, 1)
+    x_first(2)
     x_forward(1)
-    x_first(2)
     ring_step(2, 0)
-    x_forward(2)
     for copy in loads[:3]:
         copy.wait()
     for copy in w_copies:
         copy.wait_recv()
     x_first(3)
+    x_forward(2)
     ring_step(2, 1)
     feed(x, True)
     x_forward(3)
@@ -333,14 +333,12 @@
         x_copy(g, 5, x2, 1, right).wait_recv()
     feed(x2, False)
 
-    row_dots = jnp.zeros((ROWS, 1), F32)
     for p in range(2):
         active, slope = silu_pair(acc[3 * p])
         up, grad_hidden = acc[3 * p + 1], acc[3 * p + 2]
         hid[p] = (active * up).astype(BF16)
         gg[p] = (grad_hidden * up * slope).astype(BF16)
         gu[p] = (grad_hidden * active).astype(BF16)
-        row_dots = row_dots + jnp.sum(hid[p].astype(F32) * grad_hidden, axis=1, keepdims=True)
 
     repeat = one_hot(iota((MAIN, HALF), 1) == iota((MAIN, HALF), 0) // 8)
 
@@ -404,6 +402,11 @@
     rs_start(1)
     ring_step(4, 1)
 
+    rs_forward(0)
+    rs_free(1)
+    rs_start(2)
+
+    row_dots = jnp.sum(hid[0].astype(F32) * acc[2] + hid[1].astype(F32) * acc[5], axis=1, keepdims=True)
     n_high, n_low = halves(jnp.broadcast_to(row_dots[MAIN:], (HALF, 128)))
     m_high, m_low = halves(jnp.broadcast_to(row_dots[:MAIN], (MAIN, 128)))
     lane = iota((MAIN, 128), 1) // 32
@@ -413,18 +416,15 @@
     put(ret_s, produce(x))
     a2a(dot_s, lambda k: dot_r.at[k], o_send, o_recv, 0, HALF, -1)
 
-    rs_forward(0)
-    rs_free(1)
-    rs_start(2)
     rs_forward(1)
     rs_free(2)
     rs_start(3)
-    rs_forward(2)
-    rs_free(3)
 
     drain(shw.at[0:4], ra_recv.at[6])
     drain(shw.at[0:4], la_recv.at[7])
     give_back(0)
+    rs_forward(2)
+    rs_free(3)
     give_back(1)
 
     own_slot = peer_of(iota((HALF, MAIN), 1) // 8) == iota((HALF, MAIN), 0)
@@ -482,16 +482,33 @@
         return remote(src, dst, s_send.at[n], s_recv.at[n], dp, t)
 
     top, low_ = slice(0, 64), slice(64, TOK)
-    sh_s[0] = shared_out(x2).astype(BF16)
+    def own_half(v):
+        low = jnp.concatenate([v[:, 0:EIGHTH], v[:, QUARTER : QUARTER + EIGHTH]], axis=1)
+        high = jnp.concatenate([v[:, EIGHTH:QUARTER], v[:, QUARTER + EIGHTH :]], axis=1)
+        return jnp.where(c == 0, low, high), jnp.where(c == 0, high, low)
+
+    pair = []
+    for n, q in enumerate((x2, x1, x3, x)):
+        kept, given = own_half(shared_out(q))
+        keep[n] = kept
+        ps_s[n] = given.astype(BF16)
+        pair.append(remote(ps_s.at[n], ps_r.at[n], ps_send.at[n], ps_recv.at[n], dp, x * 2 + 1 - c))
+        go(pair[n])
+
+    def pair_sum(n):
+        pair[n].wait_recv()
+        return keep[n] + ps_r[n].astype(F32)
+
+    sh_s[0] = pair_sum(0).astype(BF16)
     go(s_copy(0, sh_s.at[0, top], sh_r.at[0, top], right))
     go(s_copy(1, sh_s.at[0, low_], sh_r.at[0, low_], left))
-    sh_s[1] = shared_out(x1).astype(BF16)
+    sh_s[1] = pair_sum(1).astype(BF16)
     go(s_copy(2, sh_s.at[1, low_], sh_r.at[1, low_], right))
-    sh_s[2] = shared_out(x3).astype(BF16)
+    sh_s[2] = pair_sum(2).astype(BF16)
     go(s_copy(3, sh_s.at[2, top], sh_r.at[2, top], left))
+    shared_own = pair_sum(3)
 
     give_back(3)
-    total = shared_out(x)
 
     s_copy(0, sh_s.at[0, top], sh_r.at[0, top], left).wait_recv()
     add_part(sh_s, (1, top), sh_r[0, top])
@@ -530,23 +547,20 @@
     s_copy(3, sh_s.at[2, top], sh_r.at[2, top], right).wait_recv()
     s_copy(4, sh_s.at[1, top], sh_r.at[1, top], left).wait_recv()
     s_copy(5, sh_s.at[2, low_], sh_r.at[2, low_], right).wait_recv()
-    total = total + sh_r[1].astype(F32) + sh_r[2].astype(F32)
+    shared_own = shared_own + sh_r[1].astype(F32) + sh_r[2].astype(F32)
 
     for g in range(SETS):
         drain(ret_r.at[0:8], t_recv.at[g])
     unpack_into(xrow, ret_r[...])
-    total = total + mm(main_high, xrow[0:MAIN, :]) + mm(main_low, xrow[0:MAIN, :])
+    total = mm(main_high, xrow[0:MAIN, :]) + mm(main_low, xrow[0:MAIN, :])
     total = total + mm(nine_high, xrow[MAIN:ROWS, :]) + mm(nine_low, xrow[MAIN:ROWS, :])
-    low = jnp.concatenate([total[:, 0:EIGHTH], total[:, QUARTER : QUARTER + EIGHTH]], axis=1)
-    high = jnp.concatenate([total[:, EIGHTH:QUARTER], total[:, QUARTER + EIGHTH :]], axis=1)
-    px_s[...] = jnp.where(c == 0, high, low)
-    own = jnp.where(c == 0, low, high)
+    own, px_s[...] = own_half(total)
     px = remote(px_s, px_r, px_sem.at[0], px_sem.at[1], dp, x * 2 + 1 - c)
     px.start()
     px.wait_recv()
-    both = own + px_r[...]
-    result[:, :EIGHTH] = both[:, :EIGHTH]
-    result[:, EIGHTH:] = both[:, EIGHTH:] + grad
+    both = own + px_r[...] + shared_own
+    result[:, :EIGHTH] = both[:, :EIGHTH].astype(BF16)
+    result[:, EIGHTH:] = (both[:, EIGHTH:] + grad).astype(BF16)
 
     a2a_sent(send, d_send)
     a2a_sent(ret_s, t_send)
@@ -573,7 +587,7 @@
     block = (HALF, 8, PACK)
     sums = pl.pallas_call(
         body,
-        out_shape=jax.ShapeDtypeStruct((TOK, QUARTER), F32),
+        out_shape=jax.ShapeDtypeStruct((TOK, QUARTER), BF16),
         in_specs=[vmem] * 9 + [hbm] * 3,
         out_specs=vmem,
         scratch_shapes=[
@@ -597,8 +611,11 @@
             pltpu.VMEM((RING * RING, 32, 3 * SPAD), BF16),
             pltpu.VMEM((32, 3 * SPAD), BF16),
             pltpu.VMEM((1, WIDTH), F32),
-            pltpu.VMEM((3, TOK, 2 * QUARTER), BF16),
-            pltpu.VMEM((3, TOK, 2 * QUARTER), BF16),
+            pltpu.VMEM((3, TOK, QUARTER), BF16),
+            pltpu.VMEM((3, TOK, QUARTER), BF16),
+            pltpu.VMEM((4, TOK, QUARTER), F32),
+            pltpu.VMEM((4, TOK, QUARTER), BF16),
+            pltpu.VMEM((4, TOK, QUARTER), BF16),
             pltpu.VMEM((TOK, QUARTER), F32),
             pltpu.VMEM((TOK, QUARTER), F32),
             pltpu.VMEM((HALF, TOK), F32),
@@ -610,7 +627,7 @@
             pltpu.VMEM((8, 8, TOK), F32),
             dma((4,)), dma((3,)), dma((3,)), dma, dma((4,)), dma((24,)), dma((24,)), dma((24,)), dma((24,)),
             dma, dma((4,)), dma((4,)), dma((4,)), dma((4,)), dma((4,)), dma((8,)), dma((8,)), dma((8,)), dma((8,)),
-            dma((6,)), dma((6,)), dma((2,)), dma, dma, dma, dma, dma, dma,
+            dma((6,)), dma((6,)), dma((2,)), dma, dma, dma, dma, dma, dma, dma((4,)), dma((4,)),
         ],
         compiler_params=pltpu.CompilerParams(
             collective_id=0, has_side_effects=True, vmem_limit_bytes=60 * 1024 * 1024
@@ -620,7 +637,7 @@
         sh_gate, sh_up, sh_down.T,
         ex_gate.reshape(WIDTH, HID).T, ex_up.reshape(WIDTH, HID).T, ex_down.reshape(HID, WIDTH),
     )
-    return sums[:, :EIGHTH].astype(BF16), sums[:, EIGHTH:].astype(BF16)
+    return sums[:, :EIGHTH], sums[:, EIGHTH:]
 
 
 def solution(mesh):

time: 94.9 us -> 92.9 us (0.979)
  Pallas kernels: 92.5 us -> 90.6 us
  other arithmetic: 0.97 us -> 0 us
    pallas_call x1, Pallas kernels: 92.5 us -> 90.6 us  [shards(): pl.pallas_call(body, out_shape=jax.ShapeDtypeStruct((TOK, QUARTER), BF16)...]
    another operation x1 -> x0, other arithmetic: 0.97 us -> none
where the time goes in v4:
time: 92.9 us; the launch traced here: 92.7 us
  Pallas kernels  90.6 us (98%)
  local copies, waits for them, and re-layouts  1.53 us (2%)
    pallas_call x1, Pallas kernels, shards(): pl.pallas_call(body, out_shape=jax.ShapeDtypeStruct((TOK, QUARTER), BF16)...  90.6 us

profile of v4, /device:TPU:1, one launch (start us, length us, event | category | flops | bytes accessed | tf_op | source)
XLA Modules:
  0.0 92.7 jit_solution(2498127000459713547)
XLA Ops:
  0.6 90.6 %shard_map.131 = bf16[128,512]{1,0:T(8,128)(2,1)} custom-call(bf16[128,2048]{1,0:T(8,128)(2,1)} %tok.1, bf16[128,2048]{1,0:T(8,128)(2,1)} %cot.1, s32[4,128]{1,0:T(4,128)} %bitcast.18, s32[1,60]{1,0:T(1,128)} %bitcast.19, bf16[60,2048]{1,0:T(8,128)(2,1)} %bitcast.15, bf16[16,128]{1,0:T(8,128)(2,1)} %bitcast.17, bf16[32,352]{1,0:T(8,128)(2,1)} %sh_gate.1, ...), custom_call_target="tpu_custom_call" | custom-call | tf_op jit(solution)/shard_map/pallas_call | solution.py:588
  91.2 1.5 %fusion = (bf16[128,256]{1,0:T(8,128)(2,1)}, bf16[128,256]{1,0:T(8,128)(2,1)}) fusion(bf16[128,512]{1,0:T(8,128)(2,1)} %shard_map.131), kind=kLoop, calls=%fused_computation | loop fusion | bytes 262144 | tf_op jit(solution)/shard_map/slice | solution.py:640
